TPU v7x, 32 devices: a whole 2x2x4 slice. The times are simulated.
32 devices in a mesh: data: 2 (over x), ffn: 4 (over z), hid: 4 (over y, core).
Axes of the slice: x: 2, y: 2, z: 4, core: 2. Of those that a mesh axis runs over, the one named last changes fastest.
Arguments:
- x_in: bfloat16 [128, 3072], P('data', 'hid'), parts along dimension 0
- gain_one: float32 [3072], P('hid')
- gain_two: float32 [3072], P('hid')
- w_gate: bfloat16 [3072, 24576], P('hid', 'ffn')
- w_up: bfloat16 [3072, 24576], P('hid', 'ffn')
- w_down: bfloat16 [24576, 3072], P('ffn', 'hid')
- w_qkv: bfloat16 [3072, 12288], P('hid', 'ffn')
- dx_out: bfloat16 [128, 3072], P('data', 'hid'), parts along dimension 0
- d_qkv: bfloat16 [128, 12288], P('data', 'ffn'), parts along dimension 0
Outputs:
- output 1: bfloat16 [128, 3072], P('data', 'hid'), parts along dimension 0
- output 2: bfloat16 [6144, 24576], P(('data', 'hid'), 'ffn'), parts along dimension 0
- output 3: bfloat16 [6144, 24576], P(('data', 'hid'), 'ffn'), parts along dimension 0
- output 4: bfloat16 [49152, 3072], P(('data', 'ffn'), 'hid'), parts along dimension 0
- output 5: bfloat16 [6144, 12288], P(('data', 'hid'), 'ffn'), parts along dimension 0
- output 6: float32 [6144], P(('data', 'hid')), parts along dimension 0
- output 7: float32 [6144], P(('data', 'hid')), parts along dimension 0
There are 2 independent parts. A program takes and returns all parts, laid end to end along the dimension named above; an argument that names none is the same for every part.
All inputs are finite; a program needn't handle non-finite values.
Results may differ from a plain program's by a relative error of at most 0.00629433.
Values are sent between devices in bfloat16 or wider.
A program may use at most 1 GiB of HBM per device.

v0:
```python
import jax
import jax.numpy as jnp
from jax import lax
from jax.sharding import PartitionSpec as P

NORM_EPS = 1e-6


def dot_nt(a_mat, b_mat):
    return lax.dot_general(a_mat, b_mat, (((1,), (1,)), ((), ())), preferred_element_type=jnp.float32)


def dot_tn(a_mat, b_mat):
    return lax.dot_general(a_mat, b_mat, (((0,), (0,)), ((), ())), preferred_element_type=jnp.float32)


def norm_forward(z_val, gain_vec, d_model):
    sq_part = jnp.sum(z_val * z_val, axis=-1, keepdims=True)
    inv_rms = lax.rsqrt(lax.psum(sq_part, "hid") / d_model + NORM_EPS)
    return inv_rms, (z_val * inv_rms * gain_vec).astype(jnp.bfloat16)


def norm_backward(z_val, gain_vec, inv_rms, d_norm, d_model):
    g_dn = gain_vec * d_norm
    dot_tok = lax.psum(jnp.sum(g_dn * z_val, axis=-1, keepdims=True), "hid")
    d_input = inv_rms * g_dn - z_val * (inv_rms ** 3) * (dot_tok / d_model)
    d_gain = jnp.sum(d_norm * z_val * inv_rms, axis=0)
    return d_input, d_gain


def solution(mesh):
    hid_size = mesh.shape["hid"]

    def local_step(x_in, gain_one, gain_two, w_gate, w_up, w_down, w_qkv, dx_out, d_qkv):
        d_model = x_in.shape[1] * hid_size
        x_f32 = x_in.astype(jnp.float32)
        inv_one, normed_one = norm_forward(x_f32, gain_one, d_model)
        gate_part = jnp.dot(normed_one, w_gate, preferred_element_type=jnp.float32)
        up_part = jnp.dot(normed_one, w_up, preferred_element_type=jnp.float32)
        gate_pre, up_pre = lax.psum((gate_part, up_part), "hid")
        gate_silu = jax.nn.silu(gate_pre)
        act_bf = (gate_silu * up_pre).astype(jnp.bfloat16)
        down_sum = lax.psum(jnp.dot(act_bf, w_down, preferred_element_type=jnp.float32), "ffn")
        resid_f32 = (x_f32 + down_sum).astype(jnp.bfloat16).astype(jnp.float32)
        inv_two, normed_two = norm_forward(resid_f32, gain_two, d_model)
        dw_qkv = dot_tn(normed_two, d_qkv).astype(jnp.bfloat16)
        d_normed_two = lax.psum(dot_nt(d_qkv, w_qkv), "ffn")
        d_resid, d_gain_two = norm_backward(resid_f32, gain_two, inv_two, d_normed_two, d_model)
        d_res_tot = dx_out.astype(jnp.float32) + d_resid
        d_res_bf = d_res_tot.astype(jnp.bfloat16)
        dw_down = dot_tn(act_bf, d_res_bf).astype(jnp.bfloat16)
        d_act = lax.psum(dot_nt(d_res_bf, w_down), "hid")
        gate_sig = jax.nn.sigmoid(gate_pre)
        d_gate = (d_act * up_pre * gate_sig * (1.0 + gate_pre * (1.0 - gate_sig))).astype(jnp.bfloat16)
        d_up = (d_act * gate_silu).astype(jnp.bfloat16)
        dw_gate = dot_tn(normed_one, d_gate).astype(jnp.bfloat16)
        dw_up = dot_tn(normed_one, d_up).astype(jnp.bfloat16)
        d_normed_one = lax.psum(dot_nt(d_gate, w_gate) + dot_nt(d_up, w_up), "ffn")
        d_in, d_gain_one = norm_backward(x_f32, gain_one, inv_one, d_normed_one, d_model)
        dx_in = (d_res_tot + d_in).astype(jnp.bfloat16)
        return dx_in, dw_gate, dw_up, dw_down, dw_qkv, d_gain_one, d_gain_two

    tok_spec = P("data", "hid")
    in_specs = (tok_spec, P("hid"), P("hid"), P("hid", "ffn"), P("hid", "ffn"), P("ffn", "hid"), P("hid", "ffn"), tok_spec, P("data", "ffn"))
    out_specs = (tok_spec, P(("data", "hid"), "ffn"), P(("data", "hid"), "ffn"), P(("data", "ffn"), "hid"), P(("data", "hid"), "ffn"), P(("data", "hid")), P(("data", "hid")))
    return jax.shard_map(local_step, mesh=mesh, in_specs=in_specs, out_specs=out_specs, check_vma=False)
```

profile of v0, /device:TPU:0, one launch (start us, length us, event | category | flops | bytes accessed | tf_op | source)
XLA Modules:
  0.0 275.9 jit_solution(12105363382081226611)
XLA Ops:
  7.2 0.0 copy-start
  7.2 0.0 all-reduce.11.cloned.1.call-start
  7.2 1.1 fusion.10
  8.3 8.4 %psum.70 = f32[64,1]{0,1:T(1,128)S(1)} all-reduce(f32[64,1]{0,1:T(1,128)S(1)} %bitcast.36), channel_id=1, replica_groups=mesh['data'=2,'ffn'=4,'hid'=4] {'hid'}, use_global_device_ids=true, to_apply=%region_1.0 | all-reduce | flops 64 | bytes 512 | tf_op jit(solution)/shard_map/psum | solution.py:19
  16.7 0.0 copy-start.5
  16.8 6.8 %fusion.33 = f32[64,6144]{1,0:T(8,128)} fusion(bf16[768,6144]{1,0:T(8,128)(2,1)} %param.13, bf16[64,768]{1,0:T(8,128)(2,1)} %param.9, f32[768]{0:T(1024)} %param.10, f32[64]{0:T(128)S(1)} %get-tuple-element.20), kind=kOutput, calls=%fused_computation.56 | convolution fusion | flops 604176384 | bytes 11111680 | tf_op jit(solution)/shard_map/dot_general | solution.py:39
  23.6 0.0 copy-done.2
  23.6 0.0 copy-done.3
  23.6 2.9 %fusion.35 = f32[64,6144]{1,0:T(8,128)} fusion(bf16[768,6144]{1,0:T(8,128)(2,1)S(1)} %copy-done.2, bf16[64,768]{1,0:T(8,128)(2,1)S(1)} %copy-done.3, f32[768]{0:T(1024)S(1)} %copy-done.5, f32[64]{0:T(128)S(1)} %get-tuple-element.20), kind=kOutput, calls=%fused_computation.57 | convolution fusion | flops 604176384 | bytes 11111680 | tf_op jit(solution)/shard_map/dot_general | solution.py:38
  26.6 0.0 all-reduce.11.cloned.1.call-update
  26.6 0.0 all-reduce.13.cloned.1.call-start
  26.6 4.6 %fusion.39 = f32[64,768]{1,0:T(8,128)} fusion(bf16[64,3072]{1,0:T(8,128)(2,1)S(1)} %copy-done, bf16[768,3072]{1,0:T(8,128)(2,1)} %param.15), kind=kOutput, calls=%fused_computation.59 | convolution fusion | flops 301989888 | bytes 5308416 | tf_op jit(solution)/shard_map/dot_general | solution.py:10
  31.2 64.1 %all-reduce.11.cloned.1.call-done = (f32[64,6144]{1,0:T(8,128)}, f32[64,6144]{1,0:T(8,128)}) async-done(((f32[64,6144]{1,0:T(8,128)}, f32[64,6144]{1,0:T(8,128)}), (f32[64,6144]{1,0:T(8,128)}, f32[64,6144]{1,0:T(8,128)})) %all-reduce.11.cloned.1.call-update) | async-done | bytes 3145744 | tf_op jit(solution)/shard_map/psum | solution.py:40
  95.3 2.3 multiply_convert_fusion.2
  97.6 0.0 copy-start.6
  97.6 0.0 copy-start.7
  97.6 6.1 %fusion.38 = f32[64,768]{1,0:T(8,128)} fusion(bf16[64,6144]{1,0:T(8,128)(2,1)S(1)} %multiply_convert_fusion.2, bf16[6144,768]{1,0:T(8,128)(2,1)} %param.14), kind=kOutput, calls=%fused_computation.58 | convolution fusion | flops 603979776 | bytes 10420224 | tf_op jit(solution)/shard_map/dot_general | solution.py:43
  103.8 0.0 all-reduce.13.cloned.1.call-update
  103.8 0.0 all-reduce.7.cloned.1.call-start
  103.8 37.5 %all-reduce.13.cloned.1.call-done = (f32[64,768]{1,0:T(8,128)}, f32[64,768]{1,0:T(8,128)}) async-done(((f32[64,768]{1,0:T(8,128)}, f32[64,768]{1,0:T(8,128)}), (f32[64,768]{1,0:T(8,128)}, f32[64,768]{1,0:T(8,128)})) %all-reduce.13.cloned.1.call-update) | async-done | bytes 393232 | tf_op jit(solution)/shard_map/psum | solution.py:43
  141.3 1.1 fusion.1
  142.4 5.7 %psum.74 = f32[64,1]{0,1:T(1,128)S(1)} all-reduce(f32[64,1]{0,1:T(1,128)S(1)} %bitcast.33), channel_id=1, replica_groups=mesh['data'=2,'ffn'=4,'hid'=4] {'hid'}, use_global_device_ids=true, to_apply=%region_6.7 | all-reduce | flops 64 | bytes 512 | tf_op jit(solution)/shard_map/psum | solution.py:19
  148.0 1.6 fusion.9
  149.6 6.6 %psum.76 = f32[64,1]{0,1:T(1,128)S(1)} all-reduce(f32[64,1]{0,1:T(1,128)S(1)} %bitcast.34), channel_id=1, replica_groups=mesh['data'=2,'ffn'=4,'hid'=4] {'hid'}, use_global_device_ids=true, to_apply=%region_9.10 | all-reduce | flops 64 | bytes 512 | tf_op jit(solution)/shard_map/psum | solution.py:25
  156.2 1.0 fusion.4
  157.3 7.8 %fusion.25 = f32[64,6144]{1,0:T(8,128)} fusion(bf16[6144,768]{1,0:T(8,128)(2,1)} %param.14, f32[64,768]{1,0:T(8,128)S(1)} %fusion.4), kind=kOutput, calls=%fused_computation.44 | convolution fusion | flops 604028928 | bytes 11206656 | tf_op jit(solution)/shard_map/dot_general | solution.py:10
  165.0 0.0 all-reduce.7.cloned.1.call-update
  165.1 0.2 all-reduce.9.cloned.1.call-start
  165.3 3.7 %convolution_convert_fusion.3 = bf16[768,3072]{1,0:T(8,128)(2,1)} fusion(bf16[64,3072]{1,0:T(8,128)(2,1)S(1)} %copy-done, bf16[64,768]{1,0:T(8,128)(2,1)S(1)} %get-tuple-element.16, f32[768]{0:T(1024)S(1)} %copy-done.6, f32[64]{0:T(128)S(1)} %get-tuple-element.22), kind=kOutput, calls=%fused_computation.3 | convolution fusion | flops 304545792 | bytes 5213440 | tf_op jit(solution)/shard_map/dot_general | solution.py:14
  169.0 5.2 %convolution_convert_fusion = bf16[6144,768]{1,0:T(8,128)(2,1)} fusion(bf16[64,6144]{1,0:T(8,128)(2,1)S(1)} %multiply_convert_fusion.2, f32[64,768]{1,0:T(8,128)S(1)} %fusion.4), kind=kOutput, calls=%fused_computation | convolution fusion | flops 608747520 | bytes 10420224 | tf_op jit(solution)/shard_map/dot_general | solution.py:14
  174.1 33.0 %all-reduce.7.cloned.1.call-done = f32[64,6144]{1,0:T(8,128)} async-done(((f32[64,6144]{1,0:T(8,128)}), f32[64,6144]{1,0:T(8,128)}) %all-reduce.7.cloned.1.call-update) | async-done | bytes 1572880 | tf_op jit(solution)/shard_map/psum | solution.py:52
  207.1 0.0 copy-done.4
  207.1 2.6 multiply_convert_fusion
  209.8 0.0 slice-start
  209.8 0.0 slice-start.1
  209.8 6.8 %fusion.40 = f32[64,768]{1,0:T(8,128)S(1)} fusion(bf16[64,6144]{1,0:T(8,128)(2,1)S(1)} %get-tuple-element.18, bf16[768,6144]{1,0:T(8,128)(2,1)} %param.12), kind=kOutput, calls=%fused_computation.60 | convolution fusion | flops 603979776 | bytes 10420224 | tf_op jit(solution)/shard_map/dot_general | solution.py:10
  216.6 0.0 slice-start.2
  216.6 5.2 %convolution_convert_fusion.2 = bf16[768,6144]{1,0:T(8,128)(2,1)} fusion(bf16[64,6144]{1,0:T(8,128)(2,1)S(1)} %get-tuple-element.18, bf16[64,768]{1,0:T(8,128)(2,1)S(1)} %copy-done.3, f32[768]{0:T(1024)S(1)} %copy-done.5, f32[64]{0:T(128)S(1)} %get-tuple-element.20), kind=kOutput, calls=%fused_computation.2 | convolution fusion | flops 608894976 | bytes 10325248 | tf_op jit(solution)/shard_map/dot_general | solution.py:14
  221.8 0.0 slice-done
  221.8 0.0 slice-done.2
  221.9 3.7 %convolution_add_fusion = f32[64,768]{1,0:T(8,128)} fusion(f32[64,768]{1,0:T(8,128)S(1)} %fusion.40, bf16[64,6144]{1,0:T(8,128)(2,1)S(1)} %get-tuple-element.17, bf16[768,6144]{1,0:T(8,128)(2,1)S(1)} %bitcast.32), kind=kOutput, calls=%fused_computation.9 | convolution fusion | flops 604028928 | bytes 10616832 | tf_op jit(solution)/shard_map/dot_general | solution.py:10
  225.5 0.0 all-reduce.9.cloned.1.call-update
  225.5 0.0 copy-start.1
  225.6 5.2 %convolution_convert_fusion.1 = bf16[768,6144]{1,0:T(8,128)(2,1)} fusion(bf16[64,6144]{1,0:T(8,128)(2,1)S(1)} %get-tuple-element.17, bf16[64,768]{1,0:T(8,128)(2,1)S(1)} %copy-done.3, f32[768]{0:T(1024)S(1)} %copy-done.5, f32[64]{0:T(128)S(1)} %get-tuple-element.20), kind=kOutput, calls=%fused_computation.1 | convolution fusion | flops 608894976 | bytes 10325248 | tf_op jit(solution)/shard_map/dot_general | solution.py:14
  230.8 29.7 %all-reduce.9.cloned.1.call-done = f32[64,768]{1,0:T(8,128)} async-done(((f32[64,768]{1,0:T(8,128)}), f32[64,768]{1,0:T(8,128)}) %all-reduce.9.cloned.1.call-update) | async-done | bytes 196624 | tf_op jit(solution)/shard_map/psum | solution.py:58
  260.5 1.6 fusion.20
  262.1 5.6 %psum.79 = f32[64,1]{0,1:T(1,128)S(1)} all-reduce(f32[64,1]{0,1:T(1,128)S(1)} %bitcast.35), channel_id=1, replica_groups=mesh['data'=2,'ffn'=4,'hid'=4] {'hid'}, use_global_device_ids=true, to_apply=%region_13.14 | all-reduce | flops 64 | bytes 512 | tf_op jit(solution)/shard_map/psum | solution.py:25
  267.7 1.7 fusion.17
  (14 shorter events, 0.1 us)
Async XLA Ops:
  7.2 19.5 %copy-start = (bf16[64,3072]{1,0:T(8,128)(2,1)S(1)}, bf16[64,3072]{1,0:T(8,128)(2,1)}, u32[]{:S(2)}) copy-start(bf16[64,3072]{1,0:T(8,128)(2,1)} %param.17) | copy-start | bytes 1179652
  7.2 88.1 %all-reduce.11.cloned.1.call-start = ((), (), s32[]{:S(2)}) async-start(), calls=%async_computation.2 | async-start | bytes 6291456 | tf_op jit(solution)/shard_map/psum | solution.py:40
  16.7 6.9 %copy-start.2 = (bf16[768,6144]{1,0:T(8,128)(2,1)S(1)}, bf16[768,6144]{1,0:T(8,128)(2,1)}, u32[]{:S(2)}) copy-start(bf16[768,6144]{1,0:T(8,128)(2,1)} %param.12) | copy-start | bytes 28311556
  16.7 6.9 %copy-start.3 = (bf16[64,768]{1,0:T(8,128)(2,1)S(1)}, bf16[64,768]{1,0:T(8,128)(2,1)}, u32[]{:S(2)}) copy-start(bf16[64,768]{1,0:T(8,128)(2,1)} %param.9) | copy-start | bytes 294916
  16.7 6.9 %copy-start.5 = (f32[768]{0:T(1024)S(1)}, f32[768]{0:T(1024)}, u32[]{:S(2)}) copy-start(f32[768]{0:T(1024)} %param.10) | copy-start | bytes 9220
  26.6 114.7 %all-reduce.13.cloned.1.call-start = ((), (), s32[]{:S(2)}) async-start(), calls=%async_computation.3 | async-start | bytes 786432 | tf_op jit(solution)/shard_map/psum | solution.py:43
  97.6 50.4 %copy-start.6 = (f32[768]{0:T(1024)S(1)}, f32[768]{0:T(1024)}, u32[]{:S(2)}) copy-start(f32[768]{0:T(1024)} %param.11) | copy-start | bytes 9220
  97.6 58.6 %copy-start.7 = (bf16[64,768]{1,0:T(8,128)(2,1)S(1)}, bf16[64,768]{1,0:T(8,128)(2,1)}, u32[]{:S(2)}) copy-start(bf16[64,768]{1,0:T(8,128)(2,1)} %param.16) | copy-start | bytes 294916
  103.8 103.3 %all-reduce.7.cloned.1.call-start = ((), (), s32[]{:S(2)}) async-start(), calls=%async_computation | async-start | bytes 3145728 | tf_op jit(solution)/shard_map/psum | solution.py:52
  165.1 95.4 %all-reduce.9.cloned.1.call-start = ((), (), s32[]{:S(2)}) async-start(), calls=%async_computation.1 | async-start | bytes 393216 | tf_op jit(solution)/shard_map/psum | solution.py:58
  169.0 38.2 %copy-start.4 = (f32[64,6144]{1,0:T(8,128)S(1)}, f32[64,6144]{1,0:T(8,128)}, u32[]{:S(2)}) copy-start(f32[64,6144]{1,0:T(8,128)} %get-tuple-element.11) | copy-start | bytes 4718596
  209.8 12.1 %slice-start = ((s8[9437184]{0:T(1024)(128)(4,1)}), s8[4194304]{0:T(1024)(128)(4,1)S(1)}, s32[]{:S(2)}) async-start(s8[9437184]{0:T(1024)(128)(4,1)} %bitcast.31), calls=%async_computation.4 | async-start | bytes 8388608
  209.8 12.1 %slice-start.1 = ((s8[9437184]{0:T(1024)(128)(4,1)}), s8[4194304]{0:T(1024)(128)(4,1)S(1)}, s32[]{:S(2)}) async-start(s8[9437184]{0:T(1024)(128)(4,1)} %bitcast.31), calls=%async_computation.5 | async-start | bytes 8388608
  216.6 5.3 %slice-start.2 = ((s8[9437184]{0:T(1024)(128)(4,1)}), s8[1048576]{0:T(1024)(128)(4,1)S(1)}, s32[]{:S(2)}) async-start(s8[9437184]{0:T(1024)(128)(4,1)} %bitcast.31), calls=%async_computation.6 | async-start | bytes 2097152
  225.5 43.9 %copy-start.1 = (bf16[64,3072]{1,0:T(8,128)(2,1)S(1)}, bf16[64,3072]{1,0:T(8,128)(2,1)}, u32[]{:S(2)}) copy-start(bf16[64,3072]{1,0:T(8,128)(2,1)} %param.17) | copy-start | bytes 1179652
Sparse Core Ops, SparseCore 0:
  26.7 68.5 all-reduce.10
  103.9 37.3 all-reduce.12
  165.2 41.9 all-reduce.6
  225.7 34.7 all-reduce.8
where the time goes:
time: 276 us
  waiting for transfers between devices  164 us (59%)
  matrix products  58 us (21%)
  blocking collectives  26.3 us (10%)
  between operations  13.9 us (5%)
  other arithmetic  13 us (5%)
    psum x1, waiting for transfers between devices, local_step(): gate_pre, up_pre = lax.psum((gate_part, up_part), 'hid')  64.1 us
    psum x1, waiting for transfers between devices, local_step(): lax.psum(jnp.dot(act_bf, w_down, preferred_element_type=jnp.float32), 'ffn')  37.5 us
    psum x1, waiting for transfers between devices, local_step(): d_act = lax.psum(dot_nt(d_res_bf, w_down), 'hid')  33 us
    psum x1, waiting for transfers between devices, local_step(): d_normed_one = lax.psum(dot_nt(d_gate, w_gate) + dot_nt(d_up, w_up), 'ffn')  29.7 us
    dot_general x4, matrix products, dot_nt(): lax.dot_general(a_mat, b_mat, (((1,), (1,)), ((), ())), preferred_element...  22.8 us
    dot_general x4, matrix products, dot_tn(): lax.dot_general(a_mat, b_mat, (((0,), (0,)), ((), ())), preferred_element...  19.3 us
    psum x2, blocking collectives, norm_forward(): inv_rms = lax.rsqrt(lax.psum(sq_part, 'hid') / d_model + NORM_EPS)  14.1 us
    psum x2, blocking collectives, norm_backward(): dot_tok = lax.psum(jnp.sum(g_dn * z_val, axis=-1, keepdims=True), 'hid')  12.2 us
  transfers between devices with their start and end apart: 4, of which 4 were waited for; matrix products, arithmetic and copies ran while one was open for 7% of the time, Pallas kernels for 0%

commit v1 on v0

v1 whole, which is shorter than its diff:
```python
import functools
import jax
import jax.numpy as jnp
from jax import lax
from jax.experimental import pallas as pl
from jax.experimental.pallas import tpu as pltpu
from jax.sharding import PartitionSpec as P

NORM_EPS = 1e-6
MESH = pl.DeviceIdType.MESH
ANY = pl.BlockSpec(memory_space=pl.ANY)
VM = pl.BlockSpec(memory_space=pltpu.VMEM)
BF = jnp.bfloat16
F32 = jnp.float32
LANES = 128


def dot_nn(a_mat, b_mat):
    return lax.dot_general(a_mat, b_mat, (((1,), (0,)), ((), ())), preferred_element_type=F32)


def dot_nt(a_mat, b_mat):
    return lax.dot_general(a_mat, b_mat, (((1,), (1,)), ((), ())), preferred_element_type=F32)


def dot_tn(a_mat, b_mat):
    return lax.dot_general(a_mat, b_mat, (((0,), (0,)), ((), ())), preferred_element_type=F32)


def step_kernel(
    dims,
    x_h, g1_ref, g2_ref, wg_h, wu_h, wd_h, wq_h, dxo_h, dq_h,
    dx_o, dg1_o, dg2_o, n1_o, dgu_o, dwq_o, dwd_o,
    xv, dxv, dqv, wqv, wgv, wuv, wdv,
    n1v, n2v, ebv, ev, acc, own1, d2s, d2r, ys, yr, gu, av,
    own2, e2s, e2r, ys2, yr2, dgu,
    dn2r, zs, zr, x2v, zs2, zr2, dn1v, st1, st2, st3, dxr,
    ld_sem, w_sem, out_sem,
    d2_ss, d2_rs, y_ss, y_rs, ag_ss, ag_rs, z_ss, z_rs, st_ss, st_rs,
):
    n_chunk, n_ffn, d_model = dims
    tokens, width = xv.shape
    rows = tokens // 4
    ffn_w = wgv.shape[1]
    cw = ffn_w // n_chunk
    tile = min(512, cw)

    hid = lax.axis_index("hid")
    ffn = lax.axis_index("ffn")
    chip, core = hid // 2, hid % 2
    core_peer = 2 * chip + (1 - core)
    chip_peer = 2 * (1 - chip) + core
    diag_peer = 2 * (1 - chip) + (1 - core)

    def true_row(block):
        return rows * (2 * ((block // 2 + core) % 2) + (block % 2 + chip) % 2)

    def rcopy(src, dst, ss, rs, dev):
        return pltpu.make_async_remote_copy(
            src_ref=src, dst_ref=dst, send_sem=ss, recv_sem=rs, device_id=dev, device_id_type=MESH)

    def load_rows(src, dst, slot):
        cps = []
        for j in range(4):
            r = pl.multiple_of(true_row(j), rows)
            cps.append(pltpu.make_async_copy(
                src.at[pl.ds(r, rows), :], dst.at[pl.ds(rows * j, rows), :], ld_sem.at[slot + j]))
        return cps

    def w_load(i):
        cols = pl.ds(i * cw, cw)
        return [
            pltpu.make_async_copy(wg_h.at[:, cols], wgv.at[:, cols], w_sem.at[0, i]),
            pltpu.make_async_copy(wu_h.at[:, cols], wuv.at[:, cols], w_sem.at[1, i]),
        ]

    def wd_load(i):
        cols = pl.ds(i * cw, cw)
        return pltpu.make_async_copy(wd_h.at[cols, :], wdv.at[cols, :], w_sem.at[2, i])

    x_cp = load_rows(x_h, xv, 0)
    dq_cp = load_rows(dq_h, dqv, 4)
    dx_cp = load_rows(dxo_h, dxv, 8)
    wq_cp = pltpu.make_async_copy(wq_h, wqv, ld_sem.at[12])
    for c in x_cp:
        c.start()
    for c in dq_cp:
        c.start()
    wq_cp.start()
    w_cps = [w_load(i) for i in range(n_chunk)]
    wd_cps = [wd_load(i) for i in range(n_chunk)]
    for i in range(min(2, n_chunk)):
        for c in w_cps[i]:
            c.start()

    barrier = pltpu.get_barrier_semaphore()
    peers = []
    for dh in range(4):
        for df in range(n_ffn):
            if dh or df:
                peers.append({"hid": (hid + dh) % 4, "ffn": (ffn + df) % n_ffn})
    for dev in peers:
        pl.semaphore_signal(barrier, inc=1, device_id=dev, device_id_type=MESH)

    lane = lax.broadcasted_iota(jnp.int32, (tokens, LANES), 1)
    row = lax.broadcasted_iota(jnp.int32, (tokens, LANES), 0)
    tok_id = rows * (2 * ((row // (2 * rows) + core) % 2) + ((row // rows) % 2 + chip) % 2) + row % rows

    for c in x_cp:
        c.wait()
    xf = xv[...].astype(F32)
    ssq = jnp.sum(xf * xf, axis=1, keepdims=True)
    st1[hid] = jnp.sum(jnp.where(lane == tok_id, ssq, 0.0), axis=0, keepdims=True)
    pl.semaphore_wait(barrier, len(peers))
    st1_cps = []
    for k, dev in enumerate((core_peer, chip_peer, diag_peer)):
        c = rcopy(st1.at[hid], st1.at[hid], st_ss.at[0, k], st_rs.at[0, hid], {"hid": dev})
        c.start()
        st1_cps.append(c)

    for c in dq_cp:
        c.wait()
    wq_cp.wait()
    for i in range(n_chunk):
        if i >= 2:
            for c in w_cps[i]:
                c.start()
    for i in range(n_chunk):
        wd_cps[i].start()
    for c in dx_cp:
        c.start()
    qk = min(768, dqv.shape[1])
    acc[...] = dot_nt(dqv[:, :qk], wqv[:, :qk])

    def dn2_body(k, _):
        cols = pl.ds(pl.multiple_of(k * qk, qk), qk)
        acc[...] += dot_nt(dqv[:, cols], wqv[:, cols])
        return 0
    lax.fori_loop(1, dqv.shape[1] // qk, dn2_body, 0)
    dn2r[ffn] = acc[...].astype(BF)
    dn2_cps = []
    for df in range(1, n_ffn):
        c = rcopy(dn2r.at[ffn], dn2r.at[ffn], z_ss.at[0, df], z_rs.at[0, ffn], {"ffn": (ffn + df) % n_ffn})
        c.start()
        dn2_cps.append(c)

    for dev in (core_peer, chip_peer, diag_peer):
        rcopy(st1.at[dev], st1.at[dev], st_ss.at[0, 0], st_rs.at[0, dev], {"hid": dev}).wait_recv()
    tot1 = (st1[0] + st1[1]) + (st1[2] + st1[3])
    mean1 = jnp.sum(jnp.where(lane == tok_id, tot1, 0.0), axis=1, keepdims=True) / d_model
    inv1 = lax.rsqrt(mean1 + NORM_EPS)
    g1v = g1_ref[...]
    g2v = g2_ref[...]
    n1v[...] = (xf * inv1 * g1v).astype(BF)
    n1_cp = pltpu.make_async_copy(n1v, n1_o, out_sem.at[n_chunk])
    n1_cp.start()

    half = 2 * rows
    sends = []

    def fwd_a(i):
        for c in w_cps[i]:
            c.wait()
        for w_ref, base in ((wgv, 0), (wuv, cw)):
            def body(t, _, w_ref=w_ref, base=base):
                p = dot_nn(n1v[...], w_ref[:, pl.ds(pl.multiple_of(i * cw + t * tile, tile), tile)])
                dst = pl.ds(pl.multiple_of(base + t * tile, tile), tile)
                own1[i, :, dst] = p[:half]
                d2s[i, :, dst] = p[half:].astype(BF)
                return 0
            lax.fori_loop(0, cw // tile, body, 0)
        c = rcopy(d2s.at[i], d2r.at[i], d2_ss.at[0, i], d2_rs.at[0, i], {"hid": core_peer})
        c.start()
        sends.append(c)

    def fwd_b(i):
        rcopy(d2s.at[i], d2r.at[i], d2_ss.at[0, i], d2_rs.at[0, i], {"hid": core_peer}).wait_recv()
        ys[i] = (own1[i, rows:half] + d2r[i, rows:half].astype(F32)).astype(BF)
        c = rcopy(ys.at[i], yr.at[i], y_ss.at[0, i], y_rs.at[0, i], {"hid": chip_peer})
        c.start()
        sends.append(c)
        gu[i] = own1[i, :rows] + d2r[i, :rows].astype(F32)

    def fwd_c(i):
        rcopy(ys.at[i], yr.at[i], y_ss.at[0, i], y_rs.at[0, i], {"hid": chip_peer}).wait_recv()
        tot = gu[i] + yr[i].astype(F32)
        gu[i] = tot
        g, u = tot[:, :cw], tot[:, cw:]
        av[i, :rows] = (jax.nn.silu(g) * u).astype(BF)
        own = av.at[i, pl.ds(0, rows)]
        c = rcopy(own, av.at[i, pl.ds(rows, rows)], ag_ss.at[0, 0, i], ag_rs.at[0, 0, i], {"hid": chip_peer})
        c.start()
        sends.append(c)
        c = rcopy(own, av.at[i, pl.ds(2 * rows, rows)], ag_ss.at[0, 1, i], ag_rs.at[0, 1, i], {"hid": core_peer})
        c.start()
        sends.append(c)

    def ag_wait(buf, ph, lvl, i):
        blk = buf.at[i, pl.ds((lvl + 1) * rows, rows)]
        rcopy(blk, blk, ag_ss.at[ph, lvl, i], ag_rs.at[ph, lvl, i], {"hid": core_peer}).wait_recv()

    def ag_forward(buf, ph, i):
        ag_wait(buf, ph, 0, i)
        c = rcopy(buf.at[i, pl.ds(rows, rows)], buf.at[i, pl.ds(3 * rows, rows)],
                  ag_ss.at[ph, 2, i], ag_rs.at[ph, 2, i], {"hid": core_peer})
        c.start()
        sends.append(c)

    def fwd_e(i):
        ag_wait(av, 0, 1, i)
        ag_wait(av, 0, 2, i)
        wd_cps[i].wait()
        p = dot_nn(av[i], wdv[i * cw:(i + 1) * cw, :])
        if i == 0:
            acc[...] = p
        else:
            acc[...] += p

    def pipeline(stages):
        last = max(lag for _, lag in stages)
        for s in range(n_chunk + last):
            for fn, lag in stages:
                if 0 <= s - lag < n_chunk:
                    fn(s - lag)

    pipeline([(fwd_a, 0), (fwd_b, 1), (fwd_c, 4), (lambda i: ag_forward(av, 0, i), 6), (fwd_e, 7)])

    def z_scatter(sb, rb, ph):
        sb[...] = acc[...].astype(BF)
        for df in range(1, n_ffn):
            to = (ffn + df) % n_ffn
            c = rcopy(sb.at[pl.ds(pl.multiple_of(rows * to, rows), rows)], rb.at[df - 1],
                      z_ss.at[ph, df], z_rs.at[ph, df], {"ffn": to})
            c.start()
            sends.append(c)

    def z_total(sb, rb, ph):
        tot = acc[pl.ds(pl.multiple_of(rows * ffn, rows), rows), :]
        for df in range(1, n_ffn):
            rcopy(rb.at[df - 1], rb.at[df - 1], z_ss.at[ph, df], z_rs.at[ph, df], {"ffn": ffn}).wait_recv()
            tot = tot + rb[df - 1].astype(F32)
        return tot

    def z_gather(buf, ph):
        mine = buf.at[pl.ds(pl.multiple_of(rows * ffn, rows), rows)]
        for df in range(1, n_ffn):
            c = rcopy(mine, mine, z_ss.at[ph, df], z_rs.at[ph, ffn], {"ffn": (ffn + df) % n_ffn})
            c.start()
            sends.append(c)

    def z_gather_wait(buf, ph):
        for df in range(1, n_ffn):
            frm = (ffn + df) % n_ffn
            blk = buf.at[pl.ds(pl.multiple_of(rows * frm, rows), rows)]
            rcopy(blk, blk, z_ss.at[ph, df], z_rs.at[ph, frm], {"ffn": frm}).wait_recv()

    def stat_send(st, k, ssq_v, c_v):
        ln = lax.broadcasted_iota(jnp.int32, (rows, LANES), 1)
        rw = lax.broadcasted_iota(jnp.int32, (rows, LANES), 0)
        tid = true_row(ffn) + rw
        val = jnp.where(ln == tid + tokens, c_v, 0.0)
        if ssq_v is not None:
            val = val + jnp.where(ln == tid, ssq_v, 0.0)
        me = hid * n_ffn + ffn
        st[me] = jnp.sum(val, axis=0, keepdims=True)
        for j, dev in enumerate(peers):
            c = rcopy(st.at[me], st.at[me], st_ss.at[k, j], st_rs.at[k, me], dev)
            c.start()
            sends.append(c)

    def stat_total(st, k):
        for j, dev in enumerate(peers):
            slot = dev["hid"] * n_ffn + dev["ffn"]
            rcopy(st.at[slot], st.at[slot], st_ss.at[k, j], st_rs.at[k, slot], dev).wait_recv()
        tot = st[0]
        for s in range(1, 4 * n_ffn):
            tot = tot + st[s]
        return tot

    z_scatter(zs, zr, 1)
    for df in range(1, n_ffn):
        frm = (ffn + df) % n_ffn
        rcopy(dn2r.at[frm], dn2r.at[frm], z_ss.at[0, df], z_rs.at[0, frm], {"ffn": frm}).wait_recv()
    dn2_tot = dn2r[0].astype(F32)
    for s in range(1, n_ffn):
        dn2_tot = dn2_tot + dn2r[s].astype(F32)
    ev[...] = dn2_tot
    my_rows = pl.ds(pl.multiple_of(rows * ffn, rows), rows)
    x2_rows = (xv[my_rows, :].astype(F32) + z_total(zs, zr, 1)).astype(BF)
    x2v[my_rows, :] = x2_rows
    z_gather(x2v, 2)
    x2_f = x2_rows.astype(F32)
    stat_send(st2, 1,
              jnp.sum(x2_f * x2_f, axis=1, keepdims=True),
              jnp.sum(g2v * x2_f * ev[my_rows, :], axis=1, keepdims=True))
    for c in dx_cp:
        c.wait()
    z_gather_wait(x2v, 2)
    tot2 = stat_total(st2, 1)
    inv2 = lax.rsqrt(jnp.sum(jnp.where(lane == tok_id, tot2, 0.0), axis=1, keepdims=True) / d_model + NORM_EPS)
    c2 = jnp.sum(jnp.where(lane == tok_id + tokens, tot2, 0.0), axis=1, keepdims=True)
    x2f = x2v[...].astype(F32)
    dn2 = ev[...]
    n2v[...] = (x2f * inv2 * g2v).astype(BF)
    e_val = dxv[...].astype(F32) + (inv2 * (g2v * dn2) - x2f * (inv2 ** 3) * (c2 / d_model))
    dg2_o[...] = jnp.sum(dn2 * x2f * inv2, axis=0, keepdims=True)
    ev[...] = e_val
    ebv[...] = e_val.astype(BF)

    def bwd_a(i):
        def body(t, _):
            p = dot_nt(ebv[...], wdv[pl.ds(pl.multiple_of(i * cw + t * tile, tile), tile), :])
            dst = pl.ds(pl.multiple_of(t * tile, tile), tile)
            own2[i, :, dst] = p[:half]
            e2s[i, :, dst] = p[half:].astype(BF)
            return 0
        lax.fori_loop(0, cw // tile, body, 0)
        c = rcopy(e2s.at[i], e2r.at[i], d2_ss.at[1, i], d2_rs.at[1, i], {"hid": core_peer})
        c.start()
        sends.append(c)

    def bwd_b(i):
        rcopy(e2s.at[i], e2r.at[i], d2_ss.at[1, i], d2_rs.at[1, i], {"hid": core_peer}).wait_recv()
        ys2[i] = (own2[i, rows:half] + e2r[i, rows:half].astype(F32)).astype(BF)
        c = rcopy(ys2.at[i], yr2.at[i], y_ss.at[1, i], y_rs.at[1, i], {"hid": chip_peer})
        c.start()
        sends.append(c)

    def bwd_c(i):
        rcopy(ys2.at[i], yr2.at[i], y_ss.at[1, i], y_rs.at[1, i], {"hid": chip_peer}).wait_recv()
        d_act = own2[i, :rows] + e2r[i, :rows].astype(F32) + yr2[i].astype(F32)
        g, u = gu[i, :, :cw], gu[i, :, cw:]
        sig = jax.nn.sigmoid(g)
        dgu[i, :rows, :cw] = (d_act * u * sig * (1.0 + g * (1.0 - sig))).astype(BF)
        dgu[i, :rows, cw:] = (d_act * (g * sig)).astype(BF)
        own = dgu.at[i, pl.ds(0, rows)]
        c = rcopy(own, dgu.at[i, pl.ds(rows, rows)], ag_ss.at[1, 0, i], ag_rs.at[1, 0, i], {"hid": chip_peer})
        c.start()
        sends.append(c)
        c = rcopy(own, dgu.at[i, pl.ds(2 * rows, rows)], ag_ss.at[1, 1, i], ag_rs.at[1, 1, i], {"hid": core_peer})
        c.start()
        sends.append(c)

    out_cps = []

    def bwd_e(i):
        ag_wait(dgu, 1, 1, i)
        ag_wait(dgu, 1, 2, i)
        c = pltpu.make_async_copy(dgu.at[i], dgu_o.at[i], out_sem.at[i])
        c.start()
        out_cps.append(c)
        cols = pl.ds(i * cw, cw)
        p = dot_nt(dgu[i, :, :cw], wgv[:, cols]) + dot_nt(dgu[i, :, cw:], wuv[:, cols])
        if i == 0:
            acc[...] = p
        else:
            acc[...] += p

    piece = min(256, cw)

    def fill_down(i):
        for t in range(cw // piece):
            r = i * cw + t * piece
            dwd_o[r:r + piece, :] = dot_tn(av[i, :, t * piece:(t + 1) * piece], ebv[...]).astype(BF)

    pipeline([(bwd_a, 0), (fill_down, 0), (bwd_b, 1), (bwd_c, 3), (lambda i: ag_forward(dgu, 1, i), 5), (bwd_e, 6)])

    z_scatter(zs2, zr2, 3)
    qt = min(512, dqv.shape[1])

    def fill_qkv(k, _):
        cols = pl.ds(pl.multiple_of(k * qt, qt), qt)
        dwq_o[:, cols] = dot_tn(n2v[...], dqv[:, cols]).astype(BF)
        return 0
    lax.fori_loop(0, dqv.shape[1] // qt, fill_qkv, 0)
    dn1_rows = z_total(zs2, zr2, 3).astype(BF)
    dn1v[my_rows, :] = dn1_rows
    z_gather(dn1v, 4)
    stat_send(st3, 2, None,
              jnp.sum(g1v * xv[my_rows, :].astype(F32) * dn1_rows.astype(F32), axis=1, keepdims=True))
    z_gather_wait(dn1v, 4)
    tot3 = stat_total(st3, 2)
    c1 = jnp.sum(jnp.where(lane == tok_id + tokens, tot3, 0.0), axis=1, keepdims=True)
    xf = xv[...].astype(F32)
    dn1 = dn1v[...].astype(F32)
    dxr[...] = (ev[...] + (inv1 * (g1v * dn1) - xf * (inv1 ** 3) * (c1 / d_model))).astype(BF)
    dg1_o[...] = jnp.sum(dn1 * xf * inv1, axis=0, keepdims=True)
    for j in range(4):
        r = pl.multiple_of(true_row(j), rows)
        c = pltpu.make_async_copy(dxr.at[pl.ds(rows * j, rows), :], dx_o.at[pl.ds(r, rows), :], ld_sem.at[j])
        c.start()
        out_cps.append(c)
    for c in st1_cps + dn2_cps + sends:
        c.wait_send()
    for c in out_cps:
        c.wait()
    n1_cp.wait()


def grads_kernel(n1_ref, dg_ref, du_ref, dwq_ref, dwd_ref, wg_o, wu_o, wq_o, wd_o, n1t, sem):
    step = pl.program_id(0)
    cps = (pltpu.make_async_copy(dwd_ref, wd_o, sem.at[0]), pltpu.make_async_copy(dwq_ref, wq_o, sem.at[1]))

    @pl.when(step == 0)
    def _():
        for c in cps:
            c.start()
        n1t[...] = jnp.transpose(n1_ref[...])
    wg_o[...] = dot_nn(n1t[...], dg_ref[0]).astype(BF)
    wu_o[...] = dot_nn(n1t[...], du_ref[0]).astype(BF)

    @pl.when(step == pl.num_programs(0) - 1)
    def _():
        for c in cps:
            c.wait()


def solution(mesh):
    n_hid, n_ffn = mesh.shape["hid"], mesh.shape["ffn"]

    def local_step(x_in, gain_one, gain_two, w_gate, w_up, w_down, w_qkv, dx_out, d_qkv):
        tokens, width = x_in.shape
        ffn_w, qkv_w = w_gate.shape[1], w_qkv.shape[1]
        n_chunk = 6
        cw = ffn_w // n_chunk
        rows = tokens // 4
        sds = jax.ShapeDtypeStruct
        vm = pltpu.VMEM
        dma = pltpu.SemaphoreType.DMA
        outs = pl.pallas_call(
            functools.partial(step_kernel, (n_chunk, n_ffn, width * n_hid)),
            out_shape=(
                sds((tokens, width), BF), sds((1, width), F32), sds((1, width), F32),
                sds((tokens, width), BF), sds((n_chunk, tokens, 2 * cw), BF),
                vm((width, qkv_w), BF), vm((ffn_w, width), BF),
            ),
            in_specs=[ANY, VM, VM] + [ANY] * 6,
            out_specs=(ANY, VM, VM, ANY, ANY, VM, VM),
            scratch_shapes=[
                vm((tokens, width), BF), vm((tokens, width), BF), vm((tokens, qkv_w), BF),
                vm((width, qkv_w), BF), vm((width, ffn_w), BF), vm((width, ffn_w), BF), vm((ffn_w, width), BF),
                vm((tokens, width), BF), vm((tokens, width), BF), vm((tokens, width), BF), vm((tokens, width), F32),
                vm((tokens, width), F32),
                vm((n_chunk, 2 * rows, 2 * cw), F32), vm((n_chunk, 2 * rows, 2 * cw), BF), vm((n_chunk, 2 * rows, 2 * cw), BF),
                vm((n_chunk, rows, 2 * cw), BF), vm((n_chunk, rows, 2 * cw), BF), vm((n_chunk, rows, 2 * cw), F32),
                vm((n_chunk, tokens, cw), BF),
                vm((n_chunk, 2 * rows, cw), F32), vm((n_chunk, 2 * rows, cw), BF), vm((n_chunk, 2 * rows, cw), BF),
                vm((n_chunk, rows, cw), BF), vm((n_chunk, rows, cw), BF), vm((n_chunk, tokens, 2 * cw), BF),
                vm((n_ffn, tokens, width), BF),
                vm((tokens, width), BF), vm((n_ffn - 1, rows, width), BF), vm((tokens, width), BF),
                vm((tokens, width), BF), vm((n_ffn - 1, rows, width), BF), vm((tokens, width), BF),
                vm((4, 1, LANES), F32), vm((4 * n_ffn, 1, LANES), F32), vm((4 * n_ffn, 1, LANES), F32),
                vm((tokens, width), BF),
                dma((13,)), dma((3, n_chunk)), dma((n_chunk + 1,)),
                dma((2, n_chunk)), dma((2, n_chunk)), dma((2, n_chunk)), dma((2, n_chunk)),
                dma((2, 3, n_chunk)), dma((2, 3, n_chunk)), dma((5, n_ffn)), dma((5, n_ffn)),
                dma((3, 4 * n_ffn)), dma((3, 4 * n_ffn)),
            ],
            compiler_params=pltpu.CompilerParams(
                collective_id=0, has_side_effects=True, vmem_limit_bytes=48 * 2 ** 20),
            name="block_step",
        )(x_in, gain_one.reshape(1, width), gain_two.reshape(1, width), w_gate, w_up, w_down, w_qkv, dx_out, d_qkv)
        dx_in, dg1, dg2, n1, dgu, dwq_v, dwd_v = outs
        per = max(1, cw // 512)
        tile = cw // per
        dwq_v = pltpu.with_memory_space_constraint(dwq_v, pltpu.VMEM)
        dwd_v = pltpu.with_memory_space_constraint(dwd_v, pltpu.VMEM)
        dw_gate, dw_up, dw_qkv, dw_down = pl.pallas_call(
            grads_kernel,
            grid=(n_chunk * per,),
            out_shape=(sds((width, ffn_w), BF), sds((width, ffn_w), BF), sds((width, qkv_w), BF), sds((ffn_w, width), BF)),
            in_specs=[
                pl.BlockSpec((tokens, width), lambda s: (0, 0)),
                pl.BlockSpec((1, tokens, tile), lambda s: (s // per, 0, s % per)),
                pl.BlockSpec((1, tokens, tile), lambda s: (s // per, 0, per + s % per)),
                VM, VM,
            ],
            out_specs=(
                pl.BlockSpec((width, tile), lambda s: (0, s)), pl.BlockSpec((width, tile), lambda s: (0, s)), ANY, ANY),
            scratch_shapes=[vm((width, tokens), BF), dma((2,))],
            compiler_params=pltpu.CompilerParams(vmem_limit_bytes=24 * 2 ** 20),
            name="weight_grads",
        )(n1, dgu, dgu, dwq_v, dwd_v)
        return dx_in, dw_gate, dw_up, dw_down, dw_qkv, dg1.reshape(width), dg2.reshape(width)

    tok_spec = P("data", "hid")
    in_specs = (tok_spec, P("hid"), P("hid"), P("hid", "ffn"), P("hid", "ffn"), P("ffn", "hid"), P("hid", "ffn"), tok_spec, P("data", "ffn"))
    out_specs = (tok_spec, P(("data", "hid"), "ffn"), P(("data", "hid"), "ffn"), P(("data", "ffn"), "hid"), P(("data", "hid"), "ffn"), P(("data", "hid")), P(("data", "hid")))
    return jax.shard_map(local_step, mesh=mesh, in_specs=in_specs, out_specs=out_specs, check_vma=False)
```

time: 276 us -> 95.9 us (0.35)
  waiting for transfers between devices: 164 us -> 0 us
  Pallas kernels: 0 us -> 88.2 us
  matrix products: 58 us -> 0 us
  blocking collectives: 26.3 us -> 0 us
  between operations: 13.9 us -> 0.68 us
  other arithmetic: 13 us -> 1.21 us
  local copies, waits for them, and re-layouts: 0.07 us -> 5.48 us
    psum x4 -> x0, waiting for transfers between devices: 164 us -> none  [the longest x1 64.1 us: local_step(): gate_pre, up_pre = lax.psum((gate_part, up_part), 'hid')]
    pallas_call x0 -> x2, Pallas kernels: none -> 88.2 us  [the longest x1 73.5 us: local_step(): pl.pallas_call(functools.partial(step_kernel, (n_chunk, n_ffn, width * n_...]
    dot_general x11 -> x0, matrix products: 58 us -> none  [the longest x4 22.8 us: dot_nt(): lax.dot_general(a_mat, b_mat, (((1,), (1,)), ((), ())), preferred_element...]
    psum x4 -> x0, blocking collectives: 26.3 us -> none  [the longest x2 14.1 us: norm_forward(): inv_rms = lax.rsqrt(lax.psum(sq_part, 'hid') / d_model + NORM_EPS)]
    convert_element_type x3 -> x0, other arithmetic: 6.59 us -> none  [the longest x1 2.61 us: local_step(): d_up = (d_act * gate_silu).astype(jnp.bfloat16)]
    reduce_sum x4 -> x0, other arithmetic: 5.33 us -> none  [the longest x2 3.22 us: norm_backward(): d_gain = jnp.sum(d_norm * z_val * inv_rms, axis=0)]
    unnamed x22 -> x11, local copies, waits for them, and re-layouts: 0.07 us -> 2.95 us
  transfers between devices with their start and end apart: 4 -> 0, of which waited for: 4 -> 0; matrix products, arithmetic and copies ran while one was open for 7% -> 0% of each run, Pallas kernels for 0% -> 0%
where the time goes in v1:
time: 95.9 us; the launch traced here: 95.6 us
  Pallas kernels  88.2 us (92%)
  local copies, waits for them, and re-layouts  5.48 us (6%)
  other arithmetic  1.21 us (1%)
    pallas_call x1, Pallas kernels, local_step(): pl.pallas_call(functools.partial(step_kernel, (n_chunk, n_ffn, width * n_...  73.5 us
    pallas_call x1, Pallas kernels, local_step(): pl.pallas_call(grads_kernel, grid=(n_chunk * per,), out_shape=(sds((width...  14.7 us
    unnamed x11, local copies, waits for them, and re-layouts  2.95 us

profile of v1, /device:TPU:0, one launch (start us, length us, event | category | flops | bytes accessed | tf_op | source)
XLA Modules:
  0.0 95.6 jit_solution(3844661749398275068)
XLA Ops:
  0.6 1.3 %reshape.26.g1_ref = f32[1,768]{1,0:T(1,128)} reshape(f32[768]{0:T(1024)} %param.10) | data formatting | bytes 6144 | tf_op jit(solution)/shard_map/reshape | solution.py:462
  1.9 1.3 %reshape.27.g2_ref = f32[1,768]{1,0:T(1,128)} reshape(f32[768]{0:T(1024)} %param.11) | data formatting | bytes 6144 | tf_op jit(solution)/shard_map/reshape | solution.py:462
  3.2 73.5 %block_step.1 = (bf16[64,768]{1,0:T(8,128)(2,1)}, f32[1,768]{1,0:T(1,128)}, f32[1,768]{1,0:T(1,128)}, bf16[64,768]{1,0:T(8,128)(2,1)}, bf16[6,64,2048]{2,1,0:T(8...) custom-call(bf16[64,768]{1,0:T(8,128)(2,1)} %x_h.1, f32[1,768]{1,0:T(1,128)} %reshape.26.g1_ref, ...), custom_call_target="tpu_custom_call" | custom-call | tf_op jit(solution)/shard_map/block_step/pallas_call | solution.py:430
  76.7 0.0 copy-start.4
  76.7 0.0 copy-start.3
  76.7 0.0 copy-start
  76.7 1.4 %copy-done = bf16[6,64,2048]{2,1,0:T(8,128)(2,1)S(1)} copy-done((bf16[6,64,2048]{2,1,0:T(8,128)(2,1)S(1)}, bf16[6,64,2048]{2,1,0:T(8,128)(2,1)}, u32[]{:S(2)}) %copy-start) | copy-done | bytes 1572888
  78.1 0.0 copy-start.1
  78.1 0.9 copy-done.1
  79.0 0.0 copy-start.2
  79.0 14.7 %weight_grads.1 = (bf16[768,6144]{1,0:T(8,128)(2,1)}, bf16[768,6144]{1,0:T(8,128)(2,1)}, bf16[768,3072]{1,0:T(8,128)(2,1)}, bf16[6144,768]{1,0:T(8,128)(2,1)}) custom-call(bf16[64,768]{1,0:T(8,128)(2,1)S(1)} %copy-done.1, bf16[6,64,2048]{2,1,0:T(8,128)(2,1)S(1)} %copy-done, bf16[6,64,2048]{2,1,0:T(8,128)(2,1)S(1)} %copy-done, ...), custom_call_target="tpu_custom_call" | custom-call | tf_op jit(solution)/shard_map/weight_grads/pallas_call | solution.py:468
  93.7 0.0 copy-done.4
  93.8 0.6 reduce
  94.4 0.0 copy-done.3
  94.4 0.6 reduce.1
  95.0 0.0 copy-done.2
  95.0 0.6 copy.17
Async XLA Ops:
  76.7 17.1 %copy-start.4 = (f32[1,768]{1,0:T(1,128)S(1)}, f32[1,768]{1,0:T(1,128)}, u32[]{:S(2)}) copy-start(f32[1,768]{1,0:T(1,128)} %get-tuple-element.27) | copy-start | bytes 9220
  76.7 17.7 %copy-start.3 = (f32[1,768]{1,0:T(1,128)S(1)}, f32[1,768]{1,0:T(1,128)}, u32[]{:S(2)}) copy-start(f32[1,768]{1,0:T(1,128)} %get-tuple-element.28) | copy-start | bytes 9220
  76.7 1.4 %copy-start = (bf16[6,64,2048]{2,1,0:T(8,128)(2,1)S(1)}, bf16[6,64,2048]{2,1,0:T(8,128)(2,1)}, u32[]{:S(2)}) copy-start(bf16[6,64,2048]{2,1,0:T(8,128)(2,1)} %get-tuple-element.20.dg_ref.du_ref) | copy-start | bytes 4718596
  78.1 0.9 copy-start.1
  79.0 16.0 %copy-start.2 = (bf16[64,768]{1,0:T(8,128)(2,1)S(1)}, bf16[64,768]{1,0:T(8,128)(2,1)}, u32[]{:S(2)}) copy-start(bf16[64,768]{1,0:T(8,128)(2,1)} %get-tuple-element.36) | copy-start | bytes 294916

commit v2 on v0

v2 whole, which is shorter than its diff:
```python
import functools
import jax
import jax.numpy as jnp
from jax import lax
from jax.experimental import pallas as pl
from jax.experimental.pallas import tpu as pltpu
from jax.sharding import PartitionSpec as P

NORM_EPS = 1e-6
MESH = pl.DeviceIdType.MESH
ANY = pl.BlockSpec(memory_space=pl.ANY)
VM = pl.BlockSpec(memory_space=pltpu.VMEM)
BF = jnp.bfloat16
F32 = jnp.float32
LANES = 128
N_CHUNK = 12


def dot_nn(a_mat, b_mat):
    return lax.dot_general(a_mat, b_mat, (((1,), (0,)), ((), ())), preferred_element_type=F32)


def dot_nt(a_mat, b_mat):
    return lax.dot_general(a_mat, b_mat, (((1,), (1,)), ((), ())), preferred_element_type=F32)


def dot_tn(a_mat, b_mat):
    return lax.dot_general(a_mat, b_mat, (((0,), (0,)), ((), ())), preferred_element_type=F32)


class Place:
    def __init__(self, tokens, n_ffn):
        self.tokens, self.rows, self.n_ffn = tokens, tokens // 4, n_ffn
        self.hid = lax.axis_index("hid")
        self.ffn = lax.axis_index("ffn")
        self.chip, self.core = self.hid // 2, self.hid % 2
        self.core_peer = 2 * self.chip + (1 - self.core)
        self.chip_peer = 2 * (1 - self.chip) + self.core
        self.diag_peer = 2 * (1 - self.chip) + (1 - self.core)
        self.peers = []
        for dh in range(4):
            for df in range(n_ffn):
                if dh or df:
                    self.peers.append({"hid": (self.hid + dh) % 4, "ffn": (self.ffn + df) % n_ffn})

    def true_row(self, block):
        return self.rows * (2 * ((block // 2 + self.core) % 2) + (block % 2 + self.chip) % 2)

    def my_rows(self, ffn=None):
        return pl.ds(pl.multiple_of(self.rows * (self.ffn if ffn is None else ffn), self.rows), self.rows)

    def lanes(self):
        lane = lax.broadcasted_iota(jnp.int32, (self.tokens, LANES), 1)
        row = lax.broadcasted_iota(jnp.int32, (self.tokens, LANES), 0)
        rows = self.rows
        tok = rows * (2 * ((row // (2 * rows) + self.core) % 2) + ((row // rows) % 2 + self.chip) % 2) + row % rows
        return lane, tok

    def signal_all(self, barrier):
        for dev in self.peers:
            pl.semaphore_signal(barrier, inc=1, device_id=dev, device_id_type=MESH)


def rcopy(src, dst, ss, rs, dev):
    return pltpu.make_async_remote_copy(
        src_ref=src, dst_ref=dst, send_sem=ss, recv_sem=rs, device_id=dev, device_id_type=MESH)


def z_scatter(pos, part, sb, rb, ss, rs, sends):
    sb[...] = part[...].astype(BF)
    for df in range(1, pos.n_ffn):
        to = (pos.ffn + df) % pos.n_ffn
        c = rcopy(sb.at[pos.my_rows(to)], rb.at[df - 1], ss.at[df], rs.at[df], {"ffn": to})
        c.start()
        sends.append(c)


def z_total(pos, part, rb, ss, rs):
    tot = part[pos.my_rows(), :]
    for df in range(1, pos.n_ffn):
        rcopy(rb.at[df - 1], rb.at[df - 1], ss.at[df], rs.at[df], {"ffn": pos.ffn}).wait_recv()
        tot = tot + rb[df - 1].astype(F32)
    return tot


def z_gather(pos, buf, ss, rs, sends):
    mine = buf.at[pos.my_rows()]
    for df in range(1, pos.n_ffn):
        c = rcopy(mine, mine, ss.at[df], rs.at[pos.ffn], {"ffn": (pos.ffn + df) % pos.n_ffn})
        c.start()
        sends.append(c)


def z_gather_wait(pos, buf, ss, rs):
    for df in range(1, pos.n_ffn):
        frm = (pos.ffn + df) % pos.n_ffn
        blk = buf.at[pos.my_rows(frm)]
        rcopy(blk, blk, ss.at[df], rs.at[frm], {"ffn": frm}).wait_recv()


def stat_send(pos, st, ss, rs, ssq_v, c_v, sends):
    ln = lax.broadcasted_iota(jnp.int32, (pos.rows, LANES), 1)
    tid = pos.true_row(pos.ffn) + lax.broadcasted_iota(jnp.int32, (pos.rows, LANES), 0)
    val = jnp.where(ln == tid + pos.tokens, c_v, 0.0)
    if ssq_v is not None:
        val = val + jnp.where(ln == tid, ssq_v, 0.0)
    me = pos.hid * pos.n_ffn + pos.ffn
    st[me] = jnp.sum(val, axis=0, keepdims=True)
    for j, dev in enumerate(pos.peers):
        c = rcopy(st.at[me], st.at[me], ss.at[j], rs.at[me], dev)
        c.start()
        sends.append(c)


def stat_total(pos, st, ss, rs):
    for j, dev in enumerate(pos.peers):
        slot = dev["hid"] * pos.n_ffn + dev["ffn"]
        rcopy(st.at[slot], st.at[slot], ss.at[j], rs.at[slot], dev).wait_recv()
    tot = st[0]
    for s in range(1, 4 * pos.n_ffn):
        tot = tot + st[s]
    return tot


def step_kernel(
    dims,
    x_h, g1_ref, g2_ref, wg_h, wu_h, wd_h, wq_h, dxo_h, dq_h,
    wg, wu, wd, wq, dx_o, dg1_o, dg2_o,
    xv, ev, dxv, dqv, n1v, n1t, n2v, n2t, ebv, acc, own1, d2s, d2r, ys, yr, gu, av,
    own2, e2s, e2r, ys2, yr2, dgu,
    dn2r, zs, zr, x2v, zs2, zr2, dn1v, st1, st2, st3,
    ld_sem, w_sem,
    d2_ss, d2_rs, y_ss, y_rs, ag_ss, ag_rs, z_ss, z_rs, st_ss, st_rs,
):
    n_chunk, n_ffn, d_model = dims
    tokens, width = xv.shape
    rows = tokens // 4
    half = 2 * rows
    ffn_w = wg.shape[1]
    cw = ffn_w // n_chunk
    pos = Place(tokens, n_ffn)
    barrier = pltpu.get_barrier_semaphore()
    pos.signal_all(barrier)

    def load_rows(src, dst, slot):
        cps = []
        for j in range(4):
            r = pl.multiple_of(pos.true_row(j), rows)
            cps.append(pltpu.make_async_copy(
                src.at[pl.ds(r, rows), :], dst.at[pl.ds(rows * j, rows), :], ld_sem.at[slot + j]))
        return cps

    x_cp = load_rows(x_h, xv, 0)
    dq_cp = load_rows(dq_h, dqv, 4)
    dx_cp = load_rows(dxo_h, dxv, 8)
    wq_cp = pltpu.make_async_copy(wq_h, wq, ld_sem.at[12])
    for c in x_cp:
        c.start()
    for c in dq_cp:
        c.start()
    wq_cp.start()
    w_cps, wd_cps = [], []
    for i in range(n_chunk):
        cols = pl.ds(i * cw, cw)
        w_cps.append([
            pltpu.make_async_copy(wg_h.at[:, cols], wg.at[:, cols], w_sem.at[0, i]),
            pltpu.make_async_copy(wu_h.at[:, cols], wu.at[:, cols], w_sem.at[1, i]),
        ])
        wd_cps.append(pltpu.make_async_copy(wd_h.at[cols, :], wd.at[cols, :], w_sem.at[2, i]))
    first = min(4, n_chunk)
    for i in range(first):
        for c in w_cps[i]:
            c.start()

    lane, tok_id = pos.lanes()
    for c in x_cp:
        c.wait()
    xf = xv[...].astype(F32)
    ssq = jnp.sum(xf * xf, axis=1, keepdims=True)
    st1[pos.hid] = jnp.sum(jnp.where(lane == tok_id, ssq, 0.0), axis=0, keepdims=True)
    pl.semaphore_wait(barrier, len(pos.peers))
    sends = []
    for k, dev in enumerate((pos.core_peer, pos.chip_peer, pos.diag_peer)):
        c = rcopy(st1.at[pos.hid], st1.at[pos.hid], st_ss.at[0, k], st_rs.at[0, pos.hid], {"hid": dev})
        c.start()
        sends.append(c)

    for c in dq_cp:
        c.wait()
    wq_cp.wait()
    for i in range(first, n_chunk):
        for c in w_cps[i]:
            c.start()
    for i in range(n_chunk):
        wd_cps[i].start()
    for c in dx_cp:
        c.start()
    qk = min(768, dqv.shape[1])
    acc[...] = dot_nt(dqv[:, :qk], wq[:, :qk])

    def dn2_body(k, _):
        cols = pl.ds(pl.multiple_of(k * qk, qk), qk)
        acc[...] += dot_nt(dqv[:, cols], wq[:, cols])
        return 0
    lax.fori_loop(1, dqv.shape[1] // qk, dn2_body, 0)
    dn2r[pos.ffn] = acc[...].astype(BF)
    for df in range(1, n_ffn):
        c = rcopy(dn2r.at[pos.ffn], dn2r.at[pos.ffn], z_ss.at[0, df], z_rs.at[0, pos.ffn],
                  {"ffn": (pos.ffn + df) % n_ffn})
        c.start()
        sends.append(c)

    for dev in (pos.core_peer, pos.chip_peer, pos.diag_peer):
        rcopy(st1.at[dev], st1.at[dev], st_ss.at[0, 0], st_rs.at[0, dev], {"hid": dev}).wait_recv()
    tot1 = (st1[0] + st1[1]) + (st1[2] + st1[3])
    mean1 = jnp.sum(jnp.where(lane == tok_id, tot1, 0.0), axis=1, keepdims=True) / d_model
    inv1 = lax.rsqrt(mean1 + NORM_EPS)
    g1v = jnp.reshape(g1_ref[...], (1, width))
    g2v = jnp.reshape(g2_ref[...], (1, width))
    n1 = (xf * inv1 * g1v).astype(BF)
    n1v[...] = n1

    def fwd_a(i):
        for c in w_cps[i]:
            c.wait()
        for w_ref, base in ((wg, 0), (wu, cw)):
            p = dot_nn(n1v[...], w_ref[:, i * cw:(i + 1) * cw])
            own1[i, :, base:base + cw] = p[:half]
            d2s[i, :, base:base + cw] = p[half:]
        c = rcopy(d2s.at[i], d2r.at[i], d2_ss.at[0, i], d2_rs.at[0, i], {"hid": pos.core_peer})
        c.start()
        sends.append(c)

    def fwd_b(i):
        rcopy(d2s.at[i], d2r.at[i], d2_ss.at[0, i], d2_rs.at[0, i], {"hid": pos.core_peer}).wait_recv()
        ys[i] = (own1[i, rows:half] + d2r[i, rows:half]).astype(BF)
        c = rcopy(ys.at[i], yr.at[i], y_ss.at[0, i], y_rs.at[0, i], {"hid": pos.chip_peer})
        c.start()
        sends.append(c)
        gu[i] = own1[i, :rows] + d2r[i, :rows]

    def ag_start(buf, ph, i):
        own = buf.at[i, pl.ds(0, rows)]
        c = rcopy(own, buf.at[i, pl.ds(rows, rows)], ag_ss.at[ph, 0, i], ag_rs.at[ph, 0, i], {"hid": pos.chip_peer})
        c.start()
        sends.append(c)
        c = rcopy(own, buf.at[i, pl.ds(half, rows)], ag_ss.at[ph, 1, i], ag_rs.at[ph, 1, i], {"hid": pos.core_peer})
        c.start()
        sends.append(c)

    def ag_wait(buf, ph, lvl, i):
        blk = buf.at[i, pl.ds((lvl + 1) * rows, rows)]
        rcopy(blk, blk, ag_ss.at[ph, lvl, i], ag_rs.at[ph, lvl, i], {"hid": pos.core_peer}).wait_recv()

    def ag_forward(buf, ph, i):
        ag_wait(buf, ph, 0, i)
        c = rcopy(buf.at[i, pl.ds(rows, rows)], buf.at[i, pl.ds(3 * rows, rows)],
                  ag_ss.at[ph, 2, i], ag_rs.at[ph, 2, i], {"hid": pos.core_peer})
        c.start()
        sends.append(c)

    def fwd_c(i):
        rcopy(ys.at[i], yr.at[i], y_ss.at[0, i], y_rs.at[0, i], {"hid": pos.chip_peer}).wait_recv()
        tot = gu[i] + yr[i].astype(F32)
        gu[i] = tot
        g, u = tot[:, :cw], tot[:, cw:]
        av[i, :rows] = (jax.nn.silu(g) * u).astype(BF)
        ag_start(av, 0, i)

    def fwd_e(i):
        ag_wait(av, 0, 1, i)
        ag_wait(av, 0, 2, i)
        wd_cps[i].wait()
        p = dot_nn(av[i], wd[i * cw:(i + 1) * cw, :])
        if i == 0:
            acc[...] = p
        else:
            acc[...] += p

    def lagged(*stages):
        last = max(lag for _, lag in stages)
        for s in range(n_chunk + last):
            for fn, lag in stages:
                if 0 <= s - lag < n_chunk:
                    fn(s - lag)

    lagged((fwd_a, 0), (fwd_b, 2))
    n1t[...] = jnp.transpose(n1v[...])
    lagged((fwd_c, 0))
    lagged((lambda i: ag_forward(av, 0, i), 0), (fwd_e, 2))

    z_scatter(pos, acc, zs, zr, z_ss.at[1], z_rs.at[1], sends)
    for df in range(1, n_ffn):
        frm = (pos.ffn + df) % n_ffn
        rcopy(dn2r.at[frm], dn2r.at[frm], z_ss.at[0, df], z_rs.at[0, frm], {"ffn": frm}).wait_recv()
    dn2_tot = dn2r[0].astype(F32)
    for s in range(1, n_ffn):
        dn2_tot = dn2_tot + dn2r[s].astype(F32)
    ev[...] = dn2_tot
    my_rows = pos.my_rows()
    x2_rows = (xv[my_rows, :].astype(F32) + z_total(pos, acc, zr, z_ss.at[1], z_rs.at[1])).astype(BF)
    x2v[my_rows, :] = x2_rows
    z_gather(pos, x2v, z_ss.at[2], z_rs.at[2], sends)
    x2_f = x2_rows.astype(F32)
    stat_send(pos, st2, st_ss.at[1], st_rs.at[1],
              jnp.sum(x2_f * x2_f, axis=1, keepdims=True),
              jnp.sum(g2v * x2_f * ev[my_rows, :], axis=1, keepdims=True), sends)
    for c in dx_cp:
        c.wait()
    z_gather_wait(pos, x2v, z_ss.at[2], z_rs.at[2])
    tot2 = stat_total(pos, st2, st_ss.at[1], st_rs.at[1])
    lane, tok_id = pos.lanes()
    inv2 = lax.rsqrt(jnp.sum(jnp.where(lane == tok_id, tot2, 0.0), axis=1, keepdims=True) / d_model + NORM_EPS)
    c2 = jnp.sum(jnp.where(lane == tok_id + tokens, tot2, 0.0), axis=1, keepdims=True)
    x2f = x2v[...].astype(F32)
    dn2 = ev[...]
    e_val = dxv[...].astype(F32) + (inv2 * (g2v * dn2) - x2f * (inv2 ** 3) * (c2 / d_model))
    ev[...] = e_val
    ebv[...] = e_val.astype(BF)
    n2v[...] = (x2f * inv2 * g2v).astype(BF)
    dg2_o[...] = jnp.sum(dn2 * x2f * inv2, axis=0)

    def bwd_a(i):
        p = dot_nt(ebv[...], wd[i * cw:(i + 1) * cw, :])
        own2[i] = p[:half]
        e2s[i] = p[half:]
        c = rcopy(e2s.at[i], e2r.at[i], d2_ss.at[1, i], d2_rs.at[1, i], {"hid": pos.core_peer})
        c.start()
        sends.append(c)

    def bwd_b(i):
        rcopy(e2s.at[i], e2r.at[i], d2_ss.at[1, i], d2_rs.at[1, i], {"hid": pos.core_peer}).wait_recv()
        ys2[i] = (own2[i, rows:half] + e2r[i, rows:half]).astype(BF)
        c = rcopy(ys2.at[i], yr2.at[i], y_ss.at[1, i], y_rs.at[1, i], {"hid": pos.chip_peer})
        c.start()
        sends.append(c)

    def bwd_c(i):
        rcopy(ys2.at[i], yr2.at[i], y_ss.at[1, i], y_rs.at[1, i], {"hid": pos.chip_peer}).wait_recv()
        d_act = own2[i, :rows] + e2r[i, :rows] + yr2[i].astype(F32)
        g, u = gu[i, :, :cw], gu[i, :, cw:]
        sig = jax.nn.sigmoid(g)
        dgu[i, :rows, :cw] = (d_act * u * sig * (1.0 + g * (1.0 - sig))).astype(BF)
        dgu[i, :rows, cw:] = (d_act * (g * sig)).astype(BF)
        ag_start(dgu, 1, i)

    def bwd_e(i):
        ag_wait(dgu, 1, 1, i)
        ag_wait(dgu, 1, 2, i)
        cols = slice(i * cw, (i + 1) * cw)
        p = dot_nt(dgu[i, :, :cw], wg[:, cols]) + dot_nt(dgu[i, :, cw:], wu[:, cols])
        if i == 0:
            acc[...] = p
        else:
            acc[...] += p

    def fill_gate(i):
        cols = slice(i * cw, (i + 1) * cw)
        wg[:, cols] = dot_nn(n1t[...], dgu[i, :, :cw]).astype(BF)
        wu[:, cols] = dot_nn(n1t[...], dgu[i, :, cw:]).astype(BF)

    piece = min(256, cw)

    def fill_down(i):
        for t in range(cw // piece):
            r = i * cw + t * piece
            wd[r:r + piece, :] = dot_tn(av[i, :, t * piece:(t + 1) * piece], ebv[...]).astype(BF)

    qt = dqv.shape[1] // n_chunk

    def fill_qkv(i):
        cols = slice(i * qt, (i + 1) * qt)
        wq[:, cols] = dot_nn(n2t[...], dqv[:, cols]).astype(BF)

    lagged((bwd_a, 0), (bwd_b, 2))
    n2t[...] = jnp.transpose(n2v[...])
    early = n_chunk // 3
    for i in range(early):
        fill_down(i)
    for i in range(n_chunk):
        bwd_c(i)
        if early + i < n_chunk:
            fill_down(early + i)
        if i >= n_chunk // 2:
            fill_qkv(2 * (i - n_chunk // 2))
            fill_qkv(2 * (i - n_chunk // 2) + 1)
    late = n_chunk // 3
    lagged((lambda i: ag_forward(dgu, 1, i), 0), (bwd_e, 1), (lambda i: fill_gate(i - late) if i >= late else None, 1))

    z_scatter(pos, acc, zs2, zr2, z_ss.at[3], z_rs.at[3], sends)
    for i in range(n_chunk - late, n_chunk - late // 2):
        fill_gate(i)
    g1v = jnp.reshape(g1_ref[...], (1, width))
    dn1_rows = z_total(pos, acc, zr2, z_ss.at[3], z_rs.at[3]).astype(BF)
    dn1v[my_rows, :] = dn1_rows
    z_gather(pos, dn1v, z_ss.at[4], z_rs.at[4], sends)
    stat_send(pos, st3, st_ss.at[2], st_rs.at[2], None,
              jnp.sum(g1v * xv[my_rows, :].astype(F32) * dn1_rows.astype(F32), axis=1, keepdims=True), sends)
    for i in range(n_chunk - late // 2, n_chunk):
        fill_gate(i)
    z_gather_wait(pos, dn1v, z_ss.at[4], z_rs.at[4])
    tot3 = stat_total(pos, st3, st_ss.at[2], st_rs.at[2])
    lane, tok_id = pos.lanes()
    c1 = jnp.sum(jnp.where(lane == tok_id + tokens, tot3, 0.0), axis=1, keepdims=True)
    tot1 = (st1[0] + st1[1]) + (st1[2] + st1[3])
    mean1 = jnp.sum(jnp.where(lane == tok_id, tot1, 0.0), axis=1, keepdims=True) / d_model
    inv1 = lax.rsqrt(mean1 + NORM_EPS)
    xf = xv[...].astype(F32)
    dn1 = dn1v[...].astype(F32)
    dx = (ev[...] + (inv1 * (g1v * dn1) - xf * (inv1 ** 3) * (c1 / d_model))).astype(BF)
    for j in range(4):
        dx_o[pl.ds(pl.multiple_of(pos.true_row(j), rows), rows), :] = dx[rows * j:rows * (j + 1)]
    dg1_o[...] = jnp.sum(dn1 * xf * inv1, axis=0)
    for c in sends:
        c.wait_send()


def store_kernel(*refs):
    n_part = 4
    srcs, dsts, sem = refs[:7], refs[7:14], refs[14]
    cps = []
    for k in range(4):
        rows = srcs[k].shape[0] // n_part
        for j in range(n_part):
            cps.append(pltpu.make_async_copy(
                srcs[k].at[pl.ds(j * rows, rows)], dsts[k].at[pl.ds(j * rows, rows)], sem.at[k, j]))
    for k in range(4, 7):
        cps.append(pltpu.make_async_copy(srcs[k], dsts[k], sem.at[k, 0]))
    for c in cps:
        c.start()
    for c in cps:
        c.wait()


def solution(mesh):
    n_hid, n_ffn = mesh.shape["hid"], mesh.shape["ffn"]

    def local_step(x_in, gain_one, gain_two, w_gate, w_up, w_down, w_qkv, dx_out, d_qkv):
        tokens, width = x_in.shape
        ffn_w, qkv_w = w_gate.shape[1], w_qkv.shape[1]
        n_chunk = N_CHUNK
        cw = ffn_w // n_chunk
        rows = tokens // 4
        sds = jax.ShapeDtypeStruct
        vm = pltpu.VMEM
        dma = pltpu.SemaphoreType.DMA
        outs = pl.pallas_call(
            functools.partial(step_kernel, (n_chunk, n_ffn, width * n_hid)),
            out_shape=(
                vm((width, ffn_w), BF), vm((width, ffn_w), BF), vm((ffn_w, width), BF), vm((width, qkv_w), BF),
                vm((tokens, width), BF), vm((width,), F32), vm((width,), F32),
            ),
            in_specs=[ANY, VM, VM] + [ANY] * 6,
            out_specs=(VM,) * 7,
            scratch_shapes=[
                vm((tokens, width), BF), vm((tokens, width), F32), vm((tokens, width), BF), vm((tokens, qkv_w), BF),
                vm((tokens, width), BF), vm((width, tokens), BF), vm((tokens, width), BF), vm((width, tokens), BF),
                vm((tokens, width), BF), vm((tokens, width), F32),
                vm((n_chunk, 2 * rows, 2 * cw), F32), vm((n_chunk, 2 * rows, 2 * cw), F32), vm((n_chunk, 2 * rows, 2 * cw), F32),
                vm((n_chunk, rows, 2 * cw), BF), vm((n_chunk, rows, 2 * cw), BF), vm((n_chunk, rows, 2 * cw), F32),
                vm((n_chunk, tokens, cw), BF),
                vm((n_chunk, 2 * rows, cw), F32), vm((n_chunk, 2 * rows, cw), F32), vm((n_chunk, 2 * rows, cw), F32),
                vm((n_chunk, rows, cw), BF), vm((n_chunk, rows, cw), BF), vm((n_chunk, tokens, 2 * cw), BF),
                vm((n_ffn, tokens, width), BF),
                vm((tokens, width), BF), vm((n_ffn - 1, rows, width), BF), vm((tokens, width), BF),
                vm((tokens, width), BF), vm((n_ffn - 1, rows, width), BF), vm((tokens, width), BF),
                vm((4, 1, LANES), F32), vm((4 * n_ffn, 1, LANES), F32), vm((4 * n_ffn, 1, LANES), F32),
                dma((13,)), dma((3, n_chunk)),
                dma((2, n_chunk)), dma((2, n_chunk)), dma((2, n_chunk)), dma((2, n_chunk)),
                dma((2, 3, n_chunk)), dma((2, 3, n_chunk)), dma((5, n_ffn)), dma((5, n_ffn)),
                dma((3, 4 * n_ffn)), dma((3, 4 * n_ffn)),
            ],
            compiler_params=pltpu.CompilerParams(
                collective_id=0, has_side_effects=True, vmem_limit_bytes=30 * 2 ** 20),
            name="block_step",
        )(x_in, gain_one, gain_two, w_gate, w_up, w_down, w_qkv, dx_out, d_qkv)
        outs = [pltpu.with_memory_space_constraint(o, pltpu.VMEM) for o in outs]
        dw_gate, dw_up, dw_down, dw_qkv, dx_in, dg1, dg2 = pl.pallas_call(
            store_kernel,
            out_shape=tuple(sds(o.shape, o.dtype) for o in outs),
            in_specs=[VM] * 7,
            out_specs=(ANY,) * 7,
            scratch_shapes=[dma((7, 4))],
            compiler_params=pltpu.CompilerParams(vmem_limit_bytes=30 * 2 ** 20),
            name="store_grads",
        )(*outs)
        return dx_in, dw_gate, dw_up, dw_down, dw_qkv, dg1, dg2

    tok_spec = P("data", "hid")
    in_specs = (tok_spec, P("hid"), P("hid"), P("hid", "ffn"), P("hid", "ffn"), P("ffn", "hid"), P("hid", "ffn"), tok_spec, P("data", "ffn"))
    out_specs = (tok_spec, P(("data", "hid"), "ffn"), P(("data", "hid"), "ffn"), P(("data", "ffn"), "hid"), P(("data", "hid"), "ffn"), P(("data", "hid")), P(("data", "hid")))
    return jax.shard_map(local_step, mesh=mesh, in_specs=in_specs, out_specs=out_specs, check_vma=False)
```

time: 276 us -> 88.9 us (0.32)
  waiting for transfers between devices: 164 us -> 0 us
  Pallas kernels: 0 us -> 87.9 us
  matrix products: 58 us -> 0 us
  blocking collectives: 26.3 us -> 0 us
  between operations: 13.9 us -> 0.8 us
  other arithmetic: 13 us -> 0 us
    psum x4 -> x0, waiting for transfers between devices: 164 us -> none  [the longest x1 64.1 us: local_step(): gate_pre, up_pre = lax.psum((gate_part, up_part), 'hid')]
    pallas_call x0 -> x2, Pallas kernels: none -> 87.9 us  [the longest x1 76.9 us: local_step(): pl.pallas_call(functools.partial(step_kernel, (n_chunk, n_ffn, width * n_...]
    dot_general x11 -> x0, matrix products: 58 us -> none  [the longest x4 22.8 us: dot_nt(): lax.dot_general(a_mat, b_mat, (((1,), (1,)), ((), ())), preferred_element...]
    psum x4 -> x0, blocking collectives: 26.3 us -> none  [the longest x2 14.1 us: norm_forward(): inv_rms = lax.rsqrt(lax.psum(sq_part, 'hid') / d_model + NORM_EPS)]
    convert_element_type x3 -> x0, other arithmetic: 6.59 us -> none  [the longest x1 2.61 us: local_step(): d_up = (d_act * gate_silu).astype(jnp.bfloat16)]
    reduce_sum x4 -> x0, other arithmetic: 5.33 us -> none  [the longest x2 3.22 us: norm_backward(): d_gain = jnp.sum(d_norm * z_val * inv_rms, axis=0)]
  transfers between devices with their start and end apart: 4 -> 0, of which waited for: 4 -> 0; matrix products, arithmetic and copies ran while one was open for 7% -> 0% of each run, Pallas kernels for 0% -> 0%
where the time goes in v2:
time: 88.9 us; the launch traced here: 88.7 us
  Pallas kernels  87.9 us (99%)
    pallas_call x1, Pallas kernels, local_step(): pl.pallas_call(functools.partial(step_kernel, (n_chunk, n_ffn, width * n_...  76.9 us
    pallas_call x1, Pallas kernels, local_step(): pl.pallas_call(store_kernel, out_shape=tuple((sds(o.shape, o.dtype) for o...  11 us

profile of v2, /device:TPU:0, one launch (start us, length us, event | category | flops | bytes accessed | tf_op | source)
XLA Modules:
  0.0 88.7 jit_solution(14718143611954871750)
XLA Ops:
  0.6 76.9 %block_step.1 = (bf16[768,6144]{1,0:T(8,128)(2,1)S(1)}, bf16[768,6144]{1,0:T(8,128)(2,1)S(1)}, bf16[6144,768]{1,0:T(8,128)(2,1)S(1)}, bf16[768,3072]{1,0:T(8,128...) custom-call(bf16[64,768]{1,0:T(8,128)(2,1)} %x_h.1, f32[768]{0:T(1024)} %g1_ref.1, ...), custom_call_target="tpu_custom_call" | custom-call | tf_op jit(solution)/shard_map/block_step/pallas_call | solution.py:447
  77.6 11.0 %store_grads.1 = (bf16[768,6144]{1,0:T(8,128)(2,1)}, bf16[768,6144]{1,0:T(8,128)(2,1)}, bf16[6144,768]{1,0:T(8,128)(2,1)}, bf16[768,3072]{1,0:T(8,128)(2,1)}, bf...) custom-call(bf16[768,6144]{1,0:T(8,128)(2,1)S(1)} %get-tuple-element.21.refs_0_, ...), custom_call_target="tpu_custom_call" | custom-call | tf_op jit(solution)/shard_map/store_grads/pallas_call | solution.py:478

commit v3 on v2

--- a/solution.py
+++ b/solution.py
@@ -13,7 +13,7 @@
 BF = jnp.bfloat16
 F32 = jnp.float32
 LANES = 128
-N_CHUNK = 12
+N_CHUNK = 6
 
 
 def dot_nn(a_mat, b_mat):

time: 88.9 us -> 86.2 us (0.970)
  Pallas kernels: 87.9 us -> 85.1 us
    pallas_call x1, Pallas kernels: 76.9 us -> 74.1 us  [local_step(): pl.pallas_call(functools.partial(step_kernel, (n_chunk, n_ffn, width * n_...]
where the time goes in v3:
time: 86.2 us; the launch traced here: 85.9 us
  Pallas kernels  85.1 us (99%)
    pallas_call x1, Pallas kernels, local_step(): pl.pallas_call(functools.partial(step_kernel, (n_chunk, n_ffn, width * n_...  74.1 us
    pallas_call x1, Pallas kernels, local_step(): pl.pallas_call(store_kernel, out_shape=tuple((sds(o.shape, o.dtype) for o...  11 us

profile of v3, /device:TPU:0, one launch (start us, length us, event | category | flops | bytes accessed | tf_op | source)
XLA Modules:
  0.0 85.9 jit_solution(6438111619319274393)
XLA Ops:
  0.6 74.1 %block_step.1 = (bf16[768,6144]{1,0:T(8,128)(2,1)S(1)}, bf16[768,6144]{1,0:T(8,128)(2,1)S(1)}, bf16[6144,768]{1,0:T(8,128)(2,1)S(1)}, bf16[768,3072]{1,0:T(8,128...) custom-call(bf16[64,768]{1,0:T(8,128)(2,1)} %x_h.1, f32[768]{0:T(1024)} %g1_ref.1, ...), custom_call_target="tpu_custom_call" | custom-call | tf_op jit(solution)/shard_map/block_step/pallas_call | solution.py:447
  74.8 11.0 %store_grads.1 = (bf16[768,6144]{1,0:T(8,128)(2,1)}, bf16[768,6144]{1,0:T(8,128)(2,1)}, bf16[6144,768]{1,0:T(8,128)(2,1)}, bf16[768,3072]{1,0:T(8,128)(2,1)}, bf...) custom-call(bf16[768,6144]{1,0:T(8,128)(2,1)S(1)} %get-tuple-element.21.refs_0_, ...), custom_call_target="tpu_custom_call" | custom-call | tf_op jit(solution)/shard_map/store_grads/pallas_call | solution.py:478

commit v4 on v3

--- a/solution.py
+++ b/solution.py
@@ -124,10 +124,10 @@
 
 def step_kernel(
     dims,
-    x_h, g1_ref, g2_ref, wg_h, wu_h, wd_h, wq_h, dxo_h, dq_h,
+    x_h, g1_h, g2_h, wg_h, wu_h, wd_h, wq_h, dxo_h, dq_h,
     wg, wu, wd, wq, dx_o, dg1_o, dg2_o,
-    xv, ev, dxv, dqv, n1v, n1t, n2v, n2t, ebv, acc, own1, d2s, d2r, ys, yr, gu, av,
-    own2, e2s, e2r, ys2, yr2, dgu,
+    g1_ref, g2_ref, xv, ev, dxv, dqv, n1v, n1t, n2v, n2t, ebv, acc, own1, d2s, d2r, ys, yr, gu, av,
+    own2, e2s, e2r, ys2, yr2, dgu, pq, dav,
     dn2r, zs, zr, x2v, zs2, zr2, dn1v, st1, st2, st3,
     ld_sem, w_sem,
     d2_ss, d2_rs, y_ss, y_rs, ag_ss, ag_rs, z_ss, z_rs, st_ss, st_rs,
@@ -154,7 +154,8 @@
     dq_cp = load_rows(dq_h, dqv, 4)
     dx_cp = load_rows(dxo_h, dxv, 8)
     wq_cp = pltpu.make_async_copy(wq_h, wq, ld_sem.at[12])
-    for c in x_cp:
+    g_cp = [pltpu.make_async_copy(g1_h, g1_ref, ld_sem.at[13]), pltpu.make_async_copy(g2_h, g2_ref, ld_sem.at[14])]
+    for c in x_cp + g_cp:
         c.start()
     for c in dq_cp:
         c.start()
@@ -215,6 +216,8 @@
     tot1 = (st1[0] + st1[1]) + (st1[2] + st1[3])
     mean1 = jnp.sum(jnp.where(lane == tok_id, tot1, 0.0), axis=1, keepdims=True) / d_model
     inv1 = lax.rsqrt(mean1 + NORM_EPS)
+    for c in g_cp:
+        c.wait()
     g1v = jnp.reshape(g1_ref[...], (1, width))
     g2v = jnp.reshape(g2_ref[...], (1, width))
     n1 = (xf * inv1 * g1v).astype(BF)
@@ -239,12 +242,15 @@
         sends.append(c)
         gu[i] = own1[i, :rows] + d2r[i, :rows]
 
-    def ag_start(buf, ph, i):
-        own = buf.at[i, pl.ds(0, rows)]
-        c = rcopy(own, buf.at[i, pl.ds(rows, rows)], ag_ss.at[ph, 0, i], ag_rs.at[ph, 0, i], {"hid": pos.chip_peer})
-        c.start()
-        sends.append(c)
-        c = rcopy(own, buf.at[i, pl.ds(half, rows)], ag_ss.at[ph, 1, i], ag_rs.at[ph, 1, i], {"hid": pos.core_peer})
+    def ag_chip(buf, ph, i):
+        c = rcopy(buf.at[i, pl.ds(0, rows)], buf.at[i, pl.ds(rows, rows)],
+                  ag_ss.at[ph, 0, i], ag_rs.at[ph, 0, i], {"hid": pos.chip_peer})
+        c.start()
+        sends.append(c)
+
+    def ag_core(buf, ph, i):
+        c = rcopy(buf.at[i, pl.ds(0, rows)], buf.at[i, pl.ds(half, rows)],
+                  ag_ss.at[ph, 1, i], ag_rs.at[ph, 1, i], {"hid": pos.core_peer})
         c.start()
         sends.append(c)
 
@@ -262,10 +268,14 @@
     def fwd_c(i):
         rcopy(ys.at[i], yr.at[i], y_ss.at[0, i], y_rs.at[0, i], {"hid": pos.chip_peer}).wait_recv()
         tot = gu[i] + yr[i].astype(F32)
-        gu[i] = tot
         g, u = tot[:, :cw], tot[:, cw:]
-        av[i, :rows] = (jax.nn.silu(g) * u).astype(BF)
-        ag_start(av, 0, i)
+        sig = jax.nn.sigmoid(g)
+        act = g * sig
+        av[i, :rows] = (act * u).astype(BF)
+        ag_chip(av, 0, i)
+        ag_core(av, 0, i)
+        pq[i, :rows, :cw] = (u * sig * (1.0 + g * (1.0 - sig))).astype(BF)
+        pq[i, :rows, cw:] = act.astype(BF)
 
     def fwd_e(i):
         ag_wait(av, 0, 1, i)
@@ -287,9 +297,14 @@
     lagged((fwd_a, 0), (fwd_b, 2))
     n1t[...] = jnp.transpose(n1v[...])
     lagged((fwd_c, 0))
+    ahead = (2 * n_chunk) // 3
+    for i in range(ahead):
+        ag_chip(pq, 1, i)
     lagged((lambda i: ag_forward(av, 0, i), 0), (fwd_e, 2))
 
     z_scatter(pos, acc, zs, zr, z_ss.at[1], z_rs.at[1], sends)
+    for i in range(n_chunk):
+        ag_core(pq, 1, i)
     for df in range(1, n_ffn):
         frm = (pos.ffn + df) % n_ffn
         rcopy(dn2r.at[frm], dn2r.at[frm], z_ss.at[0, df], z_rs.at[0, frm], {"ffn": frm}).wait_recv()
@@ -305,6 +320,8 @@
     stat_send(pos, st2, st_ss.at[1], st_rs.at[1],
               jnp.sum(x2_f * x2_f, axis=1, keepdims=True),
               jnp.sum(g2v * x2_f * ev[my_rows, :], axis=1, keepdims=True), sends)
+    for i in range(ahead, n_chunk):
+        ag_chip(pq, 1, i)
     for c in dx_cp:
         c.wait()
     z_gather_wait(pos, x2v, z_ss.at[2], z_rs.at[2])
@@ -338,15 +355,18 @@
     def bwd_c(i):
         rcopy(ys2.at[i], yr2.at[i], y_ss.at[1, i], y_rs.at[1, i], {"hid": pos.chip_peer}).wait_recv()
         d_act = own2[i, :rows] + e2r[i, :rows] + yr2[i].astype(F32)
-        g, u = gu[i, :, :cw], gu[i, :, cw:]
-        sig = jax.nn.sigmoid(g)
-        dgu[i, :rows, :cw] = (d_act * u * sig * (1.0 + g * (1.0 - sig))).astype(BF)
-        dgu[i, :rows, cw:] = (d_act * (g * sig)).astype(BF)
-        ag_start(dgu, 1, i)
+        dav[i, :rows] = d_act.astype(BF)
+        ag_chip(dav, 2, i)
+        ag_core(dav, 2, i)
 
     def bwd_e(i):
-        ag_wait(dgu, 1, 1, i)
-        ag_wait(dgu, 1, 2, i)
+        ag_wait(pq, 1, 1, i)
+        ag_wait(pq, 1, 2, i)
+        ag_wait(dav, 2, 1, i)
+        ag_wait(dav, 2, 2, i)
+        d_act = dav[i].astype(F32)
+        dgu[i, :, :cw] = (d_act * pq[i, :, :cw].astype(F32)).astype(BF)
+        dgu[i, :, cw:] = (d_act * pq[i, :, cw:].astype(F32)).astype(BF)
         cols = slice(i * cw, (i + 1) * cw)
         p = dot_nt(dgu[i, :, :cw], wg[:, cols]) + dot_nt(dgu[i, :, cw:], wu[:, cols])
         if i == 0:
@@ -373,6 +393,8 @@
         wq[:, cols] = dot_nn(n2t[...], dqv[:, cols]).astype(BF)
 
     lagged((bwd_a, 0), (bwd_b, 2))
+    for i in range(n_chunk):
+        ag_forward(pq, 1, i)
     n2t[...] = jnp.transpose(n2v[...])
     early = n_chunk // 3
     for i in range(early):
@@ -384,11 +406,10 @@
         if i >= n_chunk // 2:
             fill_qkv(2 * (i - n_chunk // 2))
             fill_qkv(2 * (i - n_chunk // 2) + 1)
-    late = n_chunk // 3
-    lagged((lambda i: ag_forward(dgu, 1, i), 0), (bwd_e, 1), (lambda i: fill_gate(i - late) if i >= late else None, 1))
+    lagged((lambda i: ag_forward(dav, 2, i), 0), (bwd_e, 1))
 
     z_scatter(pos, acc, zs2, zr2, z_ss.at[3], z_rs.at[3], sends)
-    for i in range(n_chunk - late, n_chunk - late // 2):
+    for i in range(n_chunk // 2):
         fill_gate(i)
     g1v = jnp.reshape(g1_ref[...], (1, width))
     dn1_rows = z_total(pos, acc, zr2, z_ss.at[3], z_rs.at[3]).astype(BF)
@@ -396,7 +417,7 @@
     z_gather(pos, dn1v, z_ss.at[4], z_rs.at[4], sends)
     stat_send(pos, st3, st_ss.at[2], st_rs.at[2], None,
               jnp.sum(g1v * xv[my_rows, :].astype(F32) * dn1_rows.astype(F32), axis=1, keepdims=True), sends)
-    for i in range(n_chunk - late // 2, n_chunk):
+    for i in range(n_chunk // 2, n_chunk):
         fill_gate(i)
     z_gather_wait(pos, dn1v, z_ss.at[4], z_rs.at[4])
     tot3 = stat_total(pos, st3, st_ss.at[2], st_rs.at[2])
@@ -450,10 +471,10 @@
                 vm((width, ffn_w), BF), vm((width, ffn_w), BF), vm((ffn_w, width), BF), vm((width, qkv_w), BF),
                 vm((tokens, width), BF), vm((width,), F32), vm((width,), F32),
             ),
-            in_specs=[ANY, VM, VM] + [ANY] * 6,
+            in_specs=[ANY] * 9,
             out_specs=(VM,) * 7,
             scratch_shapes=[
-                vm((tokens, width), BF), vm((tokens, width), F32), vm((tokens, width), BF), vm((tokens, qkv_w), BF),
+                vm((width,), F32), vm((width,), F32), vm((tokens, width), BF), vm((tokens, width), F32), vm((tokens, width), BF), vm((tokens, qkv_w), BF),
                 vm((tokens, width), BF), vm((width, tokens), BF), vm((tokens, width), BF), vm((width, tokens), BF),
                 vm((tokens, width), BF), vm((tokens, width), F32),
                 vm((n_chunk, 2 * rows, 2 * cw), F32), vm((n_chunk, 2 * rows, 2 * cw), F32), vm((n_chunk, 2 * rows, 2 * cw), F32),
@@ -461,13 +482,14 @@
                 vm((n_chunk, tokens, cw), BF),
                 vm((n_chunk, 2 * rows, cw), F32), vm((n_chunk, 2 * rows, cw), F32), vm((n_chunk, 2 * rows, cw), F32),
                 vm((n_chunk, rows, cw), BF), vm((n_chunk, rows, cw), BF), vm((n_chunk, tokens, 2 * cw), BF),
+                vm((n_chunk, tokens, 2 * cw), BF), vm((n_chunk, tokens, cw), BF),
                 vm((n_ffn, tokens, width), BF),
                 vm((tokens, width), BF), vm((n_ffn - 1, rows, width), BF), vm((tokens, width), BF),
                 vm((tokens, width), BF), vm((n_ffn - 1, rows, width), BF), vm((tokens, width), BF),
                 vm((4, 1, LANES), F32), vm((4 * n_ffn, 1, LANES), F32), vm((4 * n_ffn, 1, LANES), F32),
-                dma((13,)), dma((3, n_chunk)),
+                dma((15,)), dma((3, n_chunk)),
                 dma((2, n_chunk)), dma((2, n_chunk)), dma((2, n_chunk)), dma((2, n_chunk)),
-                dma((2, 3, n_chunk)), dma((2, 3, n_chunk)), dma((5, n_ffn)), dma((5, n_ffn)),
+                dma((3, 3, n_chunk)), dma((3, 3, n_chunk)), dma((5, n_ffn)), dma((5, n_ffn)),
                 dma((3, 4 * n_ffn)), dma((3, 4 * n_ffn)),
             ],
             compiler_params=pltpu.CompilerParams(

time: 86.2 us -> 83.3 us (0.966)
  Pallas kernels: 85.1 us -> 82.3 us
    pallas_call x1, Pallas kernels: 74.1 us -> 71.3 us  [local_step(): pl.pallas_call(functools.partial(step_kernel, (n_chunk, n_ffn, width * n_...]
where the time goes in v4:
time: 83.3 us; the launch traced here: 83.1 us
  Pallas kernels  82.3 us (99%)
    pallas_call x1, Pallas kernels, local_step(): pl.pallas_call(functools.partial(step_kernel, (n_chunk, n_ffn, width * n_...  71.3 us
    pallas_call x1, Pallas kernels, local_step(): pl.pallas_call(store_kernel, out_shape=tuple((sds(o.shape, o.dtype) for o...  11 us

profile of v4, /device:TPU:0, one launch (start us, length us, event | category | flops | bytes accessed | tf_op | source)
XLA Modules:
  0.0 83.1 jit_solution(4740958740993460236)
XLA Ops:
  0.6 71.3 %block_step.1 = (bf16[768,6144]{1,0:T(8,128)(2,1)S(1)}, bf16[768,6144]{1,0:T(8,128)(2,1)S(1)}, bf16[6144,768]{1,0:T(8,128)(2,1)S(1)}, bf16[768,3072]{1,0:T(8,128...) custom-call(bf16[64,768]{1,0:T(8,128)(2,1)} %x_h.1, f32[768]{0:T(1024)} %g1_h.1, ...), custom_call_target="tpu_custom_call" | custom-call | tf_op jit(solution)/shard_map/block_step/pallas_call | solution.py:468
  72.0 11.0 %store_grads.1 = (bf16[768,6144]{1,0:T(8,128)(2,1)}, bf16[768,6144]{1,0:T(8,128)(2,1)}, bf16[6144,768]{1,0:T(8,128)(2,1)}, bf16[768,3072]{1,0:T(8,128)(2,1)}, bf...) custom-call(bf16[768,6144]{1,0:T(8,128)(2,1)S(1)} %get-tuple-element.21.refs_0_, ...), custom_call_target="tpu_custom_call" | custom-call | tf_op jit(solution)/shard_map/store_grads/pallas_call | solution.py:500

commit v5 on v4

--- a/solution.py
+++ b/solution.py
@@ -14,6 +14,7 @@
 F32 = jnp.float32
 LANES = 128
 N_CHUNK = 6
+N_LATE = 4
 
 
 def dot_nn(a_mat, b_mat):
@@ -125,9 +126,9 @@
 def step_kernel(
     dims,
     x_h, g1_h, g2_h, wg_h, wu_h, wd_h, wq_h, dxo_h, dq_h,
-    wg, wu, wd, wq, dx_o, dg1_o, dg2_o,
-    g1_ref, g2_ref, xv, ev, dxv, dqv, n1v, n1t, n2v, n2t, ebv, acc, own1, d2s, d2r, ys, yr, gu, av,
-    own2, e2s, e2r, ys2, yr2, dgu, pq, dav,
+    wg, wu, wd, wq, dx_o, dg1_o, dg2_o, n1t, dgu,
+    g1_ref, g2_ref, xv, ev, dxv, dqv, n1v, n2v, n2t, ebv, acc, own1, d2s, d2r, ys, yr, gu, av,
+    own2, e2s, e2r, ys2, yr2, pq, dav,
     dn2r, zs, zr, x2v, zs2, zr2, dn1v, st1, st2, st3,
     ld_sem, w_sem,
     d2_ss, d2_rs, y_ss, y_rs, ag_ss, ag_rs, z_ss, z_rs, st_ss, st_rs,
@@ -294,7 +295,7 @@
                 if 0 <= s - lag < n_chunk:
                     fn(s - lag)
 
-    lagged((fwd_a, 0), (fwd_b, 2))
+    lagged((fwd_a, 0), (fwd_b, 1))
     n1t[...] = jnp.transpose(n1v[...])
     lagged((fwd_c, 0))
     ahead = (2 * n_chunk) // 3
@@ -403,21 +404,18 @@
         bwd_c(i)
         if early + i < n_chunk:
             fill_down(early + i)
-        if i >= n_chunk // 2:
-            fill_qkv(2 * (i - n_chunk // 2))
-            fill_qkv(2 * (i - n_chunk // 2) + 1)
     lagged((lambda i: ag_forward(dav, 2, i), 0), (bwd_e, 1))
 
     z_scatter(pos, acc, zs2, zr2, z_ss.at[3], z_rs.at[3], sends)
-    for i in range(n_chunk // 2):
-        fill_gate(i)
+    for i in range(n_chunk):
+        fill_qkv(i)
     g1v = jnp.reshape(g1_ref[...], (1, width))
     dn1_rows = z_total(pos, acc, zr2, z_ss.at[3], z_rs.at[3]).astype(BF)
     dn1v[my_rows, :] = dn1_rows
     z_gather(pos, dn1v, z_ss.at[4], z_rs.at[4], sends)
     stat_send(pos, st3, st_ss.at[2], st_rs.at[2], None,
               jnp.sum(g1v * xv[my_rows, :].astype(F32) * dn1_rows.astype(F32), axis=1, keepdims=True), sends)
-    for i in range(n_chunk // 2, n_chunk):
+    for i in range(n_chunk - N_LATE):
         fill_gate(i)
     z_gather_wait(pos, dn1v, z_ss.at[4], z_rs.at[4])
     tot3 = stat_total(pos, st3, st_ss.at[2], st_rs.at[2])
@@ -438,17 +436,26 @@
 
 def store_kernel(*refs):
     n_part = 4
-    srcs, dsts, sem = refs[:7], refs[7:14], refs[14]
+    srcs, n1t, dgu, dsts, sem, late_sem, late_buf = refs[:7], refs[7], refs[8], refs[9:16], refs[16], refs[17], refs[18]
+    n_chunk, cw = dgu.shape[0], dgu.shape[2] // 2
+    ready = (n_chunk - N_LATE) * cw
     cps = []
-    for k in range(4):
+    for k in (2, 3, 0, 1):
         rows = srcs[k].shape[0] // n_part
         for j in range(n_part):
-            cps.append(pltpu.make_async_copy(
-                srcs[k].at[pl.ds(j * rows, rows)], dsts[k].at[pl.ds(j * rows, rows)], sem.at[k, j]))
+            idx = (pl.ds(j * rows, rows), pl.ds(0, ready)) if k < 2 else (pl.ds(j * rows, rows),)
+            cps.append(pltpu.make_async_copy(srcs[k].at[idx], dsts[k].at[idx], sem.at[k, j]))
     for k in range(4, 7):
         cps.append(pltpu.make_async_copy(srcs[k], dsts[k], sem.at[k, 0]))
     for c in cps:
         c.start()
+    for j in range(N_LATE):
+        ch = n_chunk - N_LATE + j
+        for k in range(2):
+            late_buf[2 * j + k] = dot_nn(n1t[...], dgu[ch, :, k * cw:(k + 1) * cw]).astype(BF)
+            c = pltpu.make_async_copy(late_buf.at[2 * j + k], dsts[k].at[:, pl.ds(ch * cw, cw)], late_sem.at[2 * j + k])
+            c.start()
+            cps.append(c)
     for c in cps:
         c.wait()
 
@@ -470,18 +477,19 @@
             out_shape=(
                 vm((width, ffn_w), BF), vm((width, ffn_w), BF), vm((ffn_w, width), BF), vm((width, qkv_w), BF),
                 vm((tokens, width), BF), vm((width,), F32), vm((width,), F32),
+                vm((width, tokens), BF), vm((n_chunk, tokens, 2 * cw), BF),
             ),
             in_specs=[ANY] * 9,
-            out_specs=(VM,) * 7,
+            out_specs=(VM,) * 9,
             scratch_shapes=[
                 vm((width,), F32), vm((width,), F32), vm((tokens, width), BF), vm((tokens, width), F32), vm((tokens, width), BF), vm((tokens, qkv_w), BF),
-                vm((tokens, width), BF), vm((width, tokens), BF), vm((tokens, width), BF), vm((width, tokens), BF),
+                vm((tokens, width), BF), vm((tokens, width), BF), vm((width, tokens), BF),
                 vm((tokens, width), BF), vm((tokens, width), F32),
                 vm((n_chunk, 2 * rows, 2 * cw), F32), vm((n_chunk, 2 * rows, 2 * cw), F32), vm((n_chunk, 2 * rows, 2 * cw), F32),
                 vm((n_chunk, rows, 2 * cw), BF), vm((n_chunk, rows, 2 * cw), BF), vm((n_chunk, rows, 2 * cw), F32),
                 vm((n_chunk, tokens, cw), BF),
                 vm((n_chunk, 2 * rows, cw), F32), vm((n_chunk, 2 * rows, cw), F32), vm((n_chunk, 2 * rows, cw), F32),
-                vm((n_chunk, rows, cw), BF), vm((n_chunk, rows, cw), BF), vm((n_chunk, tokens, 2 * cw), BF),
+                vm((n_chunk, rows, cw), BF), vm((n_chunk, rows, cw), BF),
                 vm((n_chunk, tokens, 2 * cw), BF), vm((n_chunk, tokens, cw), BF),
                 vm((n_ffn, tokens, width), BF),
                 vm((tokens, width), BF), vm((n_ffn - 1, rows, width), BF), vm((tokens, width), BF),
@@ -499,10 +507,10 @@
         outs = [pltpu.with_memory_space_constraint(o, pltpu.VMEM) for o in outs]
         dw_gate, dw_up, dw_down, dw_qkv, dx_in, dg1, dg2 = pl.pallas_call(
             store_kernel,
-            out_shape=tuple(sds(o.shape, o.dtype) for o in outs),
-            in_specs=[VM] * 7,
+            out_shape=tuple(sds(o.shape, o.dtype) for o in outs[:7]),
+            in_specs=[VM] * 9,
             out_specs=(ANY,) * 7,
-            scratch_shapes=[dma((7, 4))],
+            scratch_shapes=[dma((7, 4)), dma((2 * N_LATE,)), vm((2 * N_LATE, width, cw), BF)],
             compiler_params=pltpu.CompilerParams(vmem_limit_bytes=30 * 2 ** 20),
             name="store_grads",
         )(*outs)

time: 83.3 us -> 81.8 us (0.982)
  Pallas kernels: 82.3 us -> 80.8 us
    pallas_call x1, Pallas kernels: 71.3 us -> 69.7 us  [local_step(): pl.pallas_call(functools.partial(step_kernel, (n_chunk, n_ffn, width * n_...]
where the time goes in v5:
time: 81.8 us; the launch traced here: 81.6 us
  Pallas kernels  80.8 us (99%)
    pallas_call x1, Pallas kernels, local_step(): pl.pallas_call(functools.partial(step_kernel, (n_chunk, n_ffn, width * n_...  69.7 us
    pallas_call x1, Pallas kernels, local_step(): pl.pallas_call(store_kernel, out_shape=tuple((sds(o.shape, o.dtype) for o...  11.1 us

profile of v5, /device:TPU:0, one launch (start us, length us, event | category | flops | bytes accessed | tf_op | source)
XLA Modules:
  0.0 81.6 jit_solution(13789797810591161276)
XLA Ops:
  0.6 69.7 %block_step.1 = (bf16[768,6144]{1,0:T(8,128)(2,1)S(1)}, bf16[768,6144]{1,0:T(8,128)(2,1)S(1)}, bf16[6144,768]{1,0:T(8,128)(2,1)S(1)}, bf16[768,3072]{1,0:T(8,128...) custom-call(bf16[64,768]{1,0:T(8,128)(2,1)} %x_h.1, ...), custom_call_target="tpu_custom_call" | custom-call | tf_op jit(solution)/shard_map/block_step/pallas_call | solution.py:475
  70.4 11.1 %store_grads.1 = (bf16[768,6144]{1,0:T(8,128)(2,1)}, bf16[768,6144]{1,0:T(8,128)(2,1)}, bf16[6144,768]{1,0:T(8,128)(2,1)}, bf16[768,3072]{1,0:T(8,128)(2,1)}, bf...) custom-call(bf16[768,6144]{1,0:T(8,128)(2,1)S(1)} %get-tuple-element.23.refs_0_, ...), custom_call_target="tpu_custom_call" | custom-call | tf_op jit(solution)/shard_map/store_grads/pallas_call | solution.py:508

commit v6 on v5

--- a/solution.py
+++ b/solution.py
@@ -38,6 +38,10 @@
         self.core_peer = 2 * self.chip + (1 - self.core)
         self.chip_peer = 2 * (1 - self.chip) + self.core
         self.diag_peer = 2 * (1 - self.chip) + (1 - self.core)
+        self.dists = list(range(1, n_ffn))
+        if n_ffn == 4:
+            far, near = 3 - (self.ffn + 1) // 2, 1 + 2 * (self.ffn // 2)
+            self.dists = [far, 6 - far - near, near]
         self.peers = []
         for dh in range(4):
             for df in range(n_ffn):
@@ -57,9 +61,12 @@
         tok = rows * (2 * ((row // (2 * rows) + self.core) % 2) + ((row // rows) % 2 + self.chip) % 2) + row % rows
         return lane, tok
 
-    def signal_all(self, barrier):
-        for dev in self.peers:
+    def signal_near(self, barrier):
+        near = [{"hid": h} for h in (self.core_peer, self.chip_peer, self.diag_peer)]
+        near += [{"ffn": (self.ffn + df) % self.n_ffn} for df in range(1, self.n_ffn)]
+        for dev in near:
             pl.semaphore_signal(barrier, inc=1, device_id=dev, device_id_type=MESH)
+        return len(near)
 
 
 def rcopy(src, dst, ss, rs, dev):
@@ -69,7 +76,7 @@
 
 def z_scatter(pos, part, sb, rb, ss, rs, sends):
     sb[...] = part[...].astype(BF)
-    for df in range(1, pos.n_ffn):
+    for df in pos.dists:
         to = (pos.ffn + df) % pos.n_ffn
         c = rcopy(sb.at[pos.my_rows(to)], rb.at[df - 1], ss.at[df], rs.at[df], {"ffn": to})
         c.start()
@@ -86,7 +93,7 @@
 
 def z_gather(pos, buf, ss, rs, sends):
     mine = buf.at[pos.my_rows()]
-    for df in range(1, pos.n_ffn):
+    for df in pos.dists:
         c = rcopy(mine, mine, ss.at[df], rs.at[pos.ffn], {"ffn": (pos.ffn + df) % pos.n_ffn})
         c.start()
         sends.append(c)
@@ -137,11 +144,11 @@
     tokens, width = xv.shape
     rows = tokens // 4
     half = 2 * rows
-    ffn_w = wg.shape[1]
+    ffn_w, qkv_w = wd.shape[0], dqv.shape[1]
     cw = ffn_w // n_chunk
     pos = Place(tokens, n_ffn)
     barrier = pltpu.get_barrier_semaphore()
-    pos.signal_all(barrier)
+    n_near = pos.signal_near(barrier)
 
     def load_rows(src, dst, slot):
         cps = []
@@ -154,7 +161,7 @@
     x_cp = load_rows(x_h, xv, 0)
     dq_cp = load_rows(dq_h, dqv, 4)
     dx_cp = load_rows(dxo_h, dxv, 8)
-    wq_cp = pltpu.make_async_copy(wq_h, wq, ld_sem.at[12])
+    wq_cp = pltpu.make_async_copy(wq_h, wq.at[:, pl.ds(0, qkv_w)], ld_sem.at[12])
     g_cp = [pltpu.make_async_copy(g1_h, g1_ref, ld_sem.at[13]), pltpu.make_async_copy(g2_h, g2_ref, ld_sem.at[14])]
     for c in x_cp + g_cp:
         c.start()
@@ -165,8 +172,8 @@
     for i in range(n_chunk):
         cols = pl.ds(i * cw, cw)
         w_cps.append([
-            pltpu.make_async_copy(wg_h.at[:, cols], wg.at[:, cols], w_sem.at[0, i]),
-            pltpu.make_async_copy(wu_h.at[:, cols], wu.at[:, cols], w_sem.at[1, i]),
+            pltpu.make_async_copy(wg_h.at[:, cols], wg.at[i, :, pl.ds(0, cw)], w_sem.at[0, i]),
+            pltpu.make_async_copy(wu_h.at[:, cols], wu.at[i, :, pl.ds(0, cw)], w_sem.at[1, i]),
         ])
         wd_cps.append(pltpu.make_async_copy(wd_h.at[cols, :], wd.at[cols, :], w_sem.at[2, i]))
     first = min(4, n_chunk)
@@ -180,7 +187,7 @@
     xf = xv[...].astype(F32)
     ssq = jnp.sum(xf * xf, axis=1, keepdims=True)
     st1[pos.hid] = jnp.sum(jnp.where(lane == tok_id, ssq, 0.0), axis=0, keepdims=True)
-    pl.semaphore_wait(barrier, len(pos.peers))
+    pl.semaphore_wait(barrier, n_near)
     sends = []
     for k, dev in enumerate((pos.core_peer, pos.chip_peer, pos.diag_peer)):
         c = rcopy(st1.at[pos.hid], st1.at[pos.hid], st_ss.at[0, k], st_rs.at[0, pos.hid], {"hid": dev})
@@ -228,7 +235,7 @@
         for c in w_cps[i]:
             c.wait()
         for w_ref, base in ((wg, 0), (wu, cw)):
-            p = dot_nn(n1v[...], w_ref[:, i * cw:(i + 1) * cw])
+            p = dot_nn(n1v[...], w_ref[i, :, :cw])
             own1[i, :, base:base + cw] = p[:half]
             d2s[i, :, base:base + cw] = p[half:]
         c = rcopy(d2s.at[i], d2r.at[i], d2_ss.at[0, i], d2_rs.at[0, i], {"hid": pos.core_peer})
@@ -368,17 +375,15 @@
         d_act = dav[i].astype(F32)
         dgu[i, :, :cw] = (d_act * pq[i, :, :cw].astype(F32)).astype(BF)
         dgu[i, :, cw:] = (d_act * pq[i, :, cw:].astype(F32)).astype(BF)
-        cols = slice(i * cw, (i + 1) * cw)
-        p = dot_nt(dgu[i, :, :cw], wg[:, cols]) + dot_nt(dgu[i, :, cw:], wu[:, cols])
+        p = dot_nt(dgu[i, :, :cw], wg[i, :, :cw]) + dot_nt(dgu[i, :, cw:], wu[i, :, :cw])
         if i == 0:
             acc[...] = p
         else:
             acc[...] += p
 
     def fill_gate(i):
-        cols = slice(i * cw, (i + 1) * cw)
-        wg[:, cols] = dot_nn(n1t[...], dgu[i, :, :cw]).astype(BF)
-        wu[:, cols] = dot_nn(n1t[...], dgu[i, :, cw:]).astype(BF)
+        wg[i, :, :cw] = dot_nn(n1t[...], dgu[i, :, :cw]).astype(BF)
+        wu[i, :, :cw] = dot_nn(n1t[...], dgu[i, :, cw:]).astype(BF)
 
     piece = min(256, cw)
 
@@ -438,13 +443,17 @@
     n_part = 4
     srcs, n1t, dgu, dsts, sem, late_sem, late_buf = refs[:7], refs[7], refs[8], refs[9:16], refs[16], refs[17], refs[18]
     n_chunk, cw = dgu.shape[0], dgu.shape[2] // 2
-    ready = (n_chunk - N_LATE) * cw
     cps = []
-    for k in (2, 3, 0, 1):
-        rows = srcs[k].shape[0] // n_part
+    for k in (2, 3):
+        rows, cols = dsts[k].shape[0] // n_part, dsts[k].shape[1]
         for j in range(n_part):
-            idx = (pl.ds(j * rows, rows), pl.ds(0, ready)) if k < 2 else (pl.ds(j * rows, rows),)
-            cps.append(pltpu.make_async_copy(srcs[k].at[idx], dsts[k].at[idx], sem.at[k, j]))
+            part = pl.ds(j * rows, rows)
+            cps.append(pltpu.make_async_copy(
+                srcs[k].at[part, pl.ds(0, cols)], dsts[k].at[part, :], sem.at[k, j]))
+    for k in range(2):
+        for ch in range(n_chunk - N_LATE):
+            cps.append(pltpu.make_async_copy(
+                srcs[k].at[ch, :, pl.ds(0, cw)], dsts[k].at[:, pl.ds(ch * cw, cw)], sem.at[k, ch]))
     for k in range(4, 7):
         cps.append(pltpu.make_async_copy(srcs[k], dsts[k], sem.at[k, 0]))
     for c in cps:
@@ -452,8 +461,8 @@
     for j in range(N_LATE):
         ch = n_chunk - N_LATE + j
         for k in range(2):
-            late_buf[2 * j + k] = dot_nn(n1t[...], dgu[ch, :, k * cw:(k + 1) * cw]).astype(BF)
-            c = pltpu.make_async_copy(late_buf.at[2 * j + k], dsts[k].at[:, pl.ds(ch * cw, cw)], late_sem.at[2 * j + k])
+            late_buf[2 * j + k, :, :cw] = dot_nn(n1t[...], dgu[ch, :, k * cw:(k + 1) * cw]).astype(BF)
+            c = pltpu.make_async_copy(late_buf.at[2 * j + k, :, pl.ds(0, cw)], dsts[k].at[:, pl.ds(ch * cw, cw)], late_sem.at[2 * j + k])
             c.start()
             cps.append(c)
     for c in cps:
@@ -475,7 +484,7 @@
         outs = pl.pallas_call(
             functools.partial(step_kernel, (n_chunk, n_ffn, width * n_hid)),
             out_shape=(
-                vm((width, ffn_w), BF), vm((width, ffn_w), BF), vm((ffn_w, width), BF), vm((width, qkv_w), BF),
+                vm((n_chunk, width, cw + LANES), BF), vm((n_chunk, width, cw + LANES), BF), vm((ffn_w, width), BF), vm((width, qkv_w + LANES), BF),
                 vm((tokens, width), BF), vm((width,), F32), vm((width,), F32),
                 vm((width, tokens), BF), vm((n_chunk, tokens, 2 * cw), BF),
             ),
@@ -501,17 +510,19 @@
                 dma((3, 4 * n_ffn)), dma((3, 4 * n_ffn)),
             ],
             compiler_params=pltpu.CompilerParams(
-                collective_id=0, has_side_effects=True, vmem_limit_bytes=30 * 2 ** 20),
+                collective_id=0, has_side_effects=True, vmem_limit_bytes=24 * 2 ** 20),
             name="block_step",
         )(x_in, gain_one, gain_two, w_gate, w_up, w_down, w_qkv, dx_out, d_qkv)
         outs = [pltpu.with_memory_space_constraint(o, pltpu.VMEM) for o in outs]
         dw_gate, dw_up, dw_down, dw_qkv, dx_in, dg1, dg2 = pl.pallas_call(
             store_kernel,
-            out_shape=tuple(sds(o.shape, o.dtype) for o in outs[:7]),
+            out_shape=(
+                sds((width, ffn_w), BF), sds((width, ffn_w), BF), sds((ffn_w, width), BF), sds((width, qkv_w), BF),
+                sds((tokens, width), BF), sds((width,), F32), sds((width,), F32)),
             in_specs=[VM] * 9,
             out_specs=(ANY,) * 7,
-            scratch_shapes=[dma((7, 4)), dma((2 * N_LATE,)), vm((2 * N_LATE, width, cw), BF)],
-            compiler_params=pltpu.CompilerParams(vmem_limit_bytes=30 * 2 ** 20),
+            scratch_shapes=[dma((7, max(4, n_chunk))), dma((2 * N_LATE,)), vm((2 * N_LATE, width, cw + LANES), BF)],
+            compiler_params=pltpu.CompilerParams(vmem_limit_bytes=24 * 2 ** 20),
             name="store_grads",
         )(*outs)
         return dx_in, dw_gate, dw_up, dw_down, dw_qkv, dg1, dg2

time: 81.8 us -> 81 us (level)
    pallas_call x1, Pallas kernels: 69.7 us -> 68.8 us  [local_step(): pl.pallas_call(functools.partial(step_kernel, (n_chunk, n_ffn, width * n_...]
where the time goes in v6:
time: 81 us; the launch traced here: 80.8 us
  Pallas kernels  80 us (99%)
    pallas_call x1, Pallas kernels, local_step(): pl.pallas_call(functools.partial(step_kernel, (n_chunk, n_ffn, width * n_...  68.8 us
    pallas_call x1, Pallas kernels, local_step(): pl.pallas_call(store_kernel, out_shape=(sds((width, ffn_w), BF), sds((wid...  11.2 us

profile of v6, /device:TPU:0, one launch (start us, length us, event | category | flops | bytes accessed | tf_op | source)
XLA Modules:
  0.0 80.8 jit_solution(7002036127332378327)
XLA Ops:
  0.6 68.8 %block_step.1 = (bf16[6,768,1152]{2,1,0:T(8,128)(2,1)S(1)}, bf16[6,768,1152]{2,1,0:T(8,128)(2,1)S(1)}, bf16[6144,768]{1,0:T(8,128)(2,1)S(1)}, bf16[768,3200]{1,0...) custom-call(bf16[64,768]{1,0:T(8,128)(2,1)} %x_h.1, ...), custom_call_target="tpu_custom_call" | custom-call | tf_op jit(solution)/shard_map/block_step/pallas_call | solution.py:484
  69.4 11.2 %store_grads.1 = (bf16[768,6144]{1,0:T(8,128)(2,1)}, bf16[768,6144]{1,0:T(8,128)(2,1)}, bf16[6144,768]{1,0:T(8,128)(2,1)}, bf16[768,3072]{1,0:T(8,128)(2,1)}, bf...) custom-call(bf16[6,768,1152]{2,1,0:T(8,128)(2,1)S(1)} %get-tuple-element.23.refs_0_, ...), custom_call_target="tpu_custom_call" | custom-call | tf_op jit(solution)/shard_map/store_grads/pallas_call | solution.py:517

commit v7 on v6

--- a/solution.py
+++ b/solution.py
@@ -43,9 +43,9 @@
             far, near = 3 - (self.ffn + 1) // 2, 1 + 2 * (self.ffn // 2)
             self.dists = [far, 6 - far - near, near]
         self.peers = []
-        for dh in range(4):
-            for df in range(n_ffn):
-                if dh or df:
+        for df in self.dists + [0]:
+            for dh in (2, 1, 3, 0):
+                if dh or not isinstance(df, int) or df:
                     self.peers.append({"hid": (self.hid + dh) % 4, "ffn": (self.ffn + df) % n_ffn})
 
     def true_row(self, block):
@@ -176,7 +176,7 @@
             pltpu.make_async_copy(wu_h.at[:, cols], wu.at[i, :, pl.ds(0, cw)], w_sem.at[1, i]),
         ])
         wd_cps.append(pltpu.make_async_copy(wd_h.at[cols, :], wd.at[cols, :], w_sem.at[2, i]))
-    first = min(4, n_chunk)
+    first = min(1, n_chunk)
     for i in range(first):
         for c in w_cps[i]:
             c.start()
@@ -197,13 +197,9 @@
     for c in dq_cp:
         c.wait()
     wq_cp.wait()
-    for i in range(first, n_chunk):
+    for i in range(first, min(3, n_chunk)):
         for c in w_cps[i]:
             c.start()
-    for i in range(n_chunk):
-        wd_cps[i].start()
-    for c in dx_cp:
-        c.start()
     qk = min(768, dqv.shape[1])
     acc[...] = dot_nt(dqv[:, :qk], wq[:, :qk])
 
@@ -234,6 +230,12 @@
     def fwd_a(i):
         for c in w_cps[i]:
             c.wait()
+        if i + 3 < n_chunk:
+            for c in w_cps[i + 3]:
+                c.start()
+        if i == n_chunk - 1:
+            for c in wd_cps + dx_cp:
+                c.start()
         for w_ref, base in ((wg, 0), (wu, cw)):
             p = dot_nn(n1v[...], w_ref[i, :, :cw])
             own1[i, :, base:base + cw] = p[:half]

time: 81 us -> 77.9 us (0.962)
  Pallas kernels: 80 us -> 77 us
    pallas_call x1, Pallas kernels: 68.8 us -> 65.7 us  [local_step(): pl.pallas_call(functools.partial(step_kernel, (n_chunk, n_ffn, width * n_...]
where the time goes in v7:
time: 77.9 us; the launch traced here: 77.8 us
  Pallas kernels  77 us (99%)
  between operations  0.8 us (1%)
    pallas_call x1, Pallas kernels, local_step(): pl.pallas_call(functools.partial(step_kernel, (n_chunk, n_ffn, width * n_...  65.7 us
    pallas_call x1, Pallas kernels, local_step(): pl.pallas_call(store_kernel, out_shape=(sds((width, ffn_w), BF), sds((wid...  11.2 us

profile of v7, /device:TPU:0, one launch (start us, length us, event | category | flops | bytes accessed | tf_op | source)
XLA Modules:
  0.0 77.8 jit_solution(13757235800145032016)
XLA Ops:
  0.6 65.7 %block_step.1 = (bf16[6,768,1152]{2,1,0:T(8,128)(2,1)S(1)}, bf16[6,768,1152]{2,1,0:T(8,128)(2,1)S(1)}, bf16[6144,768]{1,0:T(8,128)(2,1)S(1)}, bf16[768,3200]{1,0...) custom-call(bf16[64,768]{1,0:T(8,128)(2,1)} %x_h.1, ...), custom_call_target="tpu_custom_call" | custom-call | tf_op jit(solution)/shard_map/block_step/pallas_call | solution.py:486
  66.4 11.2 %store_grads.1 = (bf16[768,6144]{1,0:T(8,128)(2,1)}, bf16[768,6144]{1,0:T(8,128)(2,1)}, bf16[6144,768]{1,0:T(8,128)(2,1)}, bf16[768,3072]{1,0:T(8,128)(2,1)}, bf...) custom-call(bf16[6,768,1152]{2,1,0:T(8,128)(2,1)S(1)} %get-tuple-element.23.refs_0_, ...), custom_call_target="tpu_custom_call" | custom-call | tf_op jit(solution)/shard_map/store_grads/pallas_call | solution.py:519
